TPU v7x, 8 devices: a whole 2x2x1 slice. The times are simulated.
8 devices in a mesh: model: 2 (over z, y), data: 4 (over x, core).
Axes of the slice: x: 2, y: 2, z: 1, core: 2. Of those that a mesh axis runs over, the one named last changes fastest.
Arguments:
- dec_in: bfloat16 [64, 384, 512], P('data')
- enc_out: bfloat16 [64, 192, 512], P('data')
- grad_out: bfloat16 [64, 384, 512], P('data')
- rel_bias: bfloat16 [32, 6], P(None, 'model')
- self_q: bfloat16 [512, 384], P('data', 'model')
- self_k: bfloat16 [512, 384], P('data', 'model')
- self_v: bfloat16 [512, 384], P('data', 'model')
- self_o: bfloat16 [384, 512], P('model', 'data')
- cross_q: bfloat16 [512, 384], P('data', 'model')
- cross_k: bfloat16 [512, 384], P('data', 'model')
- cross_v: bfloat16 [512, 384], P('data', 'model')
- cross_o: bfloat16 [384, 512], P('model', 'data')
- mlp_wi_0: bfloat16 [512, 1024], P('data', 'model')
- mlp_wi_1: bfloat16 [512, 1024], P('data', 'model')
- mlp_wo: bfloat16 [1024, 512], P('model', 'data')
- norm_self: bfloat16 [512], P('data')
- norm_cross: bfloat16 [512], P('data')
- norm_mlp: bfloat16 [512], P('data')
Outputs:
- output 1: bfloat16 [64, 384, 512], P('data')
- output 2: bfloat16 [64, 384, 512], P('data')
- output 3: bfloat16 [64, 192, 512], P('data')
- output 4: float32 [32, 6], P(None, 'model')
- output 5: float32 [512, 384], P('data', 'model')
- output 6: float32 [512, 384], P('data', 'model')
- output 7: float32 [512, 384], P('data', 'model')
- output 8: float32 [384, 512], P('model', 'data')
- output 9: float32 [512, 384], P('data', 'model')
- output 10: float32 [512, 384], P('data', 'model')
- output 11: float32 [512, 384], P('data', 'model')
- output 12: float32 [384, 512], P('model', 'data')
- output 13: float32 [512, 1024], P('data', 'model')
- output 14: float32 [512, 1024], P('data', 'model')
- output 15: float32 [1024, 512], P('model', 'data')
- output 16: float32 [512], P('data')
- output 17: float32 [512], P('data')
- output 18: float32 [512], P('data')
All inputs are finite; a program needn't handle non-finite values.
Results may differ from a plain program's by a relative error of at most 0.02.
Values are sent between devices in bfloat16 or wider.
A program may use at most 1 GiB of HBM per device.

v0:
```python
import math
import jax
import jax.numpy as jnp
from jax import lax
from jax.sharding import PartitionSpec as P

EPS = 1e-6
NUM_BUCKETS = 32
MASK_VALUE = -1e9
BUCKET_EDGES = tuple(math.ceil(16 * 8.0 ** (bucket_no / 16.0)) for bucket_no in range(1, 16))


def bucket_table(seq_len):
    positions = jnp.arange(seq_len)
    rel_dist = jnp.maximum(positions[:, None] - positions[None, :], 0)
    bucket_edges = jnp.array(BUCKET_EDGES, dtype=jnp.int32)
    bucket_ids = jnp.minimum(rel_dist, 16) + jnp.sum((rel_dist[:, :, None] >= bucket_edges).astype(jnp.int32), axis=-1)
    one_hot = (bucket_ids[:, :, None] == jnp.arange(NUM_BUCKETS)).astype(jnp.bfloat16)
    return one_hot, positions[:, None] >= positions[None, :]


def gelu_tanh(pre_act):
    return jax.nn.gelu(pre_act, approximate=True)


def norm_fwd(act_in, gain_vec):
    act_f = act_in.astype(jnp.float32)
    inv_rms = lax.rsqrt(jnp.mean(act_f * act_f, axis=-1, keepdims=True) + EPS)
    unit_act = act_f * inv_rms
    return (unit_act * gain_vec.astype(jnp.float32)).astype(jnp.bfloat16), unit_act, inv_rms


def norm_bwd(d_norm, unit_act, inv_rms, gain_vec):
    d_norm_f = d_norm.astype(jnp.float32)
    d_unit = d_norm_f * gain_vec.astype(jnp.float32)
    d_act = inv_rms * (d_unit - unit_act * jnp.mean(d_unit * unit_act, axis=-1, keepdims=True))
    return d_act, jnp.sum(d_norm_f * unit_act, axis=(0, 1))


def project(act_in, weight):
    return jnp.einsum("bsd,dhe->bshe", act_in, weight, preferred_element_type=jnp.float32).astype(jnp.bfloat16)


def back_in(d_heads, weight):
    return jnp.einsum("bshe,dhe->bsd", d_heads, weight, preferred_element_type=jnp.float32)


def in_grad(act_in, d_heads):
    grad_w = jnp.einsum("bsd,bshe->dhe", act_in, d_heads, preferred_element_type=jnp.float32)
    return grad_w.reshape(grad_w.shape[0], -1)


def out_proj(context, weight):
    return jnp.einsum("crif,ife->cre", context, weight, preferred_element_type=jnp.float32)


def out_grad(context, d_res):
    grad_w = jnp.einsum("crif,cre->ife", context, d_res, preferred_element_type=jnp.float32)
    return grad_w.reshape(-1, grad_w.shape[2])


def ctx_grad(d_res, weight):
    return jnp.einsum("cre,ife->crif", d_res, weight, preferred_element_type=jnp.float32).astype(jnp.bfloat16)


def attn_fwd(q_heads, k_heads, v_heads, pos_bias, key_mask):
    logits = jnp.einsum("bqhe,bkhe->bhqk", q_heads, k_heads, preferred_element_type=jnp.float32)
    logits = jnp.where(key_mask, logits.astype(jnp.bfloat16).astype(jnp.float32) + pos_bias, MASK_VALUE)
    attn_probs = jax.nn.softmax(logits, axis=-1)
    context = jnp.einsum("bhqk,bkhe->bqhe", attn_probs.astype(jnp.bfloat16), v_heads, preferred_element_type=jnp.float32)
    return attn_probs, context.astype(jnp.bfloat16)


def attn_bwd(d_context, attn_probs, q_heads, k_heads, v_heads):
    d_probs = jnp.einsum("bqhe,bkhe->bhqk", d_context, v_heads, preferred_element_type=jnp.float32)
    d_probs = d_probs.astype(jnp.bfloat16).astype(jnp.float32)
    d_logits = attn_probs * (d_probs - jnp.sum(attn_probs * d_probs, axis=-1, keepdims=True))
    d_logits_b = d_logits.astype(jnp.bfloat16)
    d_query = jnp.einsum("bhqk,bkhe->bqhe", d_logits_b, k_heads, preferred_element_type=jnp.float32)
    d_key = jnp.einsum("bhqk,bqhe->bkhe", d_logits_b, q_heads, preferred_element_type=jnp.float32)
    d_value = jnp.einsum("bhqk,bqhe->bkhe", attn_probs.astype(jnp.bfloat16), d_context, preferred_element_type=jnp.float32)
    return d_logits, d_query.astype(jnp.bfloat16), d_key.astype(jnp.bfloat16), d_value.astype(jnp.bfloat16)


def residual(base_val, delta_val):
    return (base_val.astype(jnp.float32) + delta_val.astype(jnp.float32)).astype(jnp.bfloat16)


def gather_in(w_shard, heads_dev):
    w_full = lax.all_gather(w_shard, "data", axis=0, tiled=True)
    return w_full.reshape(w_full.shape[0], heads_dev, -1)


def gather_out(w_shard, heads_dev):
    w_full = lax.all_gather(w_shard, "data", axis=1, tiled=True)
    return w_full.reshape(heads_dev, -1, w_full.shape[1])


def gather_data(w_shard, dim_idx):
    return lax.all_gather(w_shard, "data", axis=dim_idx, tiled=True)


def model_sum(partial):
    return lax.psum(partial.astype(jnp.bfloat16), "model")


def data_scatter(grad_full, dim_idx):
    return lax.psum_scatter(grad_full, "data", scatter_dimension=dim_idx, tiled=True)


def layer_shard(dec_in, enc_out, grad_out, rel_bias, self_q, self_k, self_v, self_o, cross_q, cross_k, cross_v, cross_o, mlp_wi_0, mlp_wi_1, mlp_wo, norm_self, norm_cross, norm_mlp):
    heads_dev = rel_bias.shape[1]
    one_hot, causal = bucket_table(dec_in.shape[1])
    pos_bias = jnp.einsum("qkr,rh->hqk", one_hot, rel_bias, preferred_element_type=jnp.float32)
    gain_1 = gather_data(norm_self, 0)
    gain_2 = gather_data(norm_cross, 0)
    gain_3 = gather_data(norm_mlp, 0)

    normed_1, unit_1, inv_1 = norm_fwd(dec_in, gain_1)
    q_self = project(normed_1, gather_in(self_q, heads_dev))
    k_self = project(normed_1, gather_in(self_k, heads_dev))
    v_self = project(normed_1, gather_in(self_v, heads_dev))
    probs_self, ctx_self = attn_fwd(q_self, k_self, v_self, pos_bias, causal)
    mid_1 = residual(dec_in, model_sum(out_proj(ctx_self, gather_out(self_o, heads_dev))))

    normed_2, unit_2, inv_2 = norm_fwd(mid_1, gain_2)
    q_cross = project(normed_2, gather_in(cross_q, heads_dev))
    k_cross = project(enc_out, gather_in(cross_k, heads_dev))
    v_cross = project(enc_out, gather_in(cross_v, heads_dev))
    probs_cross, ctx_cross = attn_fwd(q_cross, k_cross, v_cross, 0.0, True)
    mid_2 = residual(mid_1, model_sum(out_proj(ctx_cross, gather_out(cross_o, heads_dev))))

    normed_3, unit_3, inv_3 = norm_fwd(mid_2, gain_3)
    pre_0 = jnp.einsum("bsd,df->bsf", normed_3, gather_data(mlp_wi_0, 0), preferred_element_type=jnp.float32).astype(jnp.bfloat16)
    pre_1 = jnp.einsum("bsd,df->bsf", normed_3, gather_data(mlp_wi_1, 0), preferred_element_type=jnp.float32).astype(jnp.bfloat16)
    gelu_0, gelu_pull = jax.vjp(gelu_tanh, pre_0.astype(jnp.float32))
    hidden = (gelu_0 * pre_1.astype(jnp.float32)).astype(jnp.bfloat16)
    mlp_part = jnp.einsum("bsf,fd->bsd", hidden, gather_data(mlp_wo, 1), preferred_element_type=jnp.float32)
    dec_out = residual(mid_2, model_sum(mlp_part))

    d_hidden = jnp.einsum("bsd,fd->bsf", grad_out, gather_data(mlp_wo, 1), preferred_element_type=jnp.float32)
    d_hidden = d_hidden.astype(jnp.bfloat16).astype(jnp.float32)
    d_pre_0 = gelu_pull(d_hidden * pre_1.astype(jnp.float32))[0].astype(jnp.bfloat16)
    d_pre_1 = (d_hidden * gelu_0).astype(jnp.bfloat16)
    d_norm_3 = model_sum(jnp.einsum("bsf,df->bsd", d_pre_0, gather_data(mlp_wi_0, 0), preferred_element_type=jnp.float32) + jnp.einsum("bsf,df->bsd", d_pre_1, gather_data(mlp_wi_1, 0), preferred_element_type=jnp.float32))
    grad_mlp_wo = data_scatter(jnp.einsum("bsf,bsd->fd", hidden, grad_out, preferred_element_type=jnp.float32), 1)
    grad_wi_0 = data_scatter(jnp.einsum("bsd,bsf->df", normed_3, d_pre_0, preferred_element_type=jnp.float32), 0)
    grad_wi_1 = data_scatter(jnp.einsum("bsd,bsf->df", normed_3, d_pre_1, preferred_element_type=jnp.float32), 0)
    d_act_3, d_gain_3 = norm_bwd(d_norm_3, unit_3, inv_3, gain_3)
    d_mid_2 = residual(grad_out, d_act_3)

    grad_cross_o = data_scatter(out_grad(ctx_cross, d_mid_2), 1)
    d_ctx_cross = ctx_grad(d_mid_2, gather_out(cross_o, heads_dev))
    _, dq_cross, dk_cross, dv_cross = attn_bwd(d_ctx_cross, probs_cross, q_cross, k_cross, v_cross)
    d_norm_2 = model_sum(back_in(dq_cross, gather_in(cross_q, heads_dev)))
    grad_enc = model_sum(back_in(dk_cross, gather_in(cross_k, heads_dev)) + back_in(dv_cross, gather_in(cross_v, heads_dev)))
    grad_cross_q = data_scatter(in_grad(normed_2, dq_cross), 0)
    grad_cross_k = data_scatter(in_grad(enc_out, dk_cross), 0)
    grad_cross_v = data_scatter(in_grad(enc_out, dv_cross), 0)
    d_act_2, d_gain_2 = norm_bwd(d_norm_2, unit_2, inv_2, gain_2)
    d_mid_1 = residual(d_mid_2, d_act_2)

    grad_self_o = data_scatter(out_grad(ctx_self, d_mid_1), 1)
    d_ctx_self = ctx_grad(d_mid_1, gather_out(self_o, heads_dev))
    d_logit_self, dq_self, dk_self, dv_self = attn_bwd(d_ctx_self, probs_self, q_self, k_self, v_self)
    bias_part = jnp.einsum("qkr,hqk->rh", one_hot.astype(jnp.float32), jnp.sum(d_logit_self, axis=0))
    grad_bias = lax.psum(bias_part, "data")
    d_norm_1 = model_sum(back_in(dq_self, gather_in(self_q, heads_dev)) + back_in(dk_self, gather_in(self_k, heads_dev)) + back_in(dv_self, gather_in(self_v, heads_dev)))
    grad_self_q = data_scatter(in_grad(normed_1, dq_self), 0)
    grad_self_k = data_scatter(in_grad(normed_1, dk_self), 0)
    grad_self_v = data_scatter(in_grad(normed_1, dv_self), 0)
    d_act_1, d_gain_1 = norm_bwd(d_norm_1, unit_1, inv_1, gain_1)
    grad_dec = residual(d_mid_1, d_act_1)
    return (dec_out, grad_dec, grad_enc, grad_bias, grad_self_q, grad_self_k, grad_self_v, grad_self_o, grad_cross_q, grad_cross_k, grad_cross_v, grad_cross_o, grad_wi_0, grad_wi_1, grad_mlp_wo, data_scatter(d_gain_1, 0), data_scatter(d_gain_2, 0), data_scatter(d_gain_3, 0))


def solution(mesh):
    row_spec = P("data", None, None)
    col_in = P("data", "model")
    col_out = P("model", "data")
    gain_spec = P("data")
    bias_spec = P(None, "model")
    arg_specs = (row_spec, row_spec, row_spec, bias_spec, col_in, col_in, col_in, col_out, col_in, col_in, col_in, col_out, col_in, col_in, col_out, gain_spec, gain_spec, gain_spec)
    out_specs = (row_spec, row_spec, row_spec) + arg_specs[3:]
    return jax.shard_map(layer_shard, mesh=mesh, in_specs=arg_specs, out_specs=out_specs, check_vma=False)
```

profile of v0, /device:TPU:0, one launch (start us, length us, event | category | flops | bytes accessed | tf_op | source)
XLA Modules:
  0.0 1595.3 jit_solution(11519740141474562836)
XLA Ops:
  8.1 9.9 all-gather
  22.7 7.8 all_gather.55
  30.6 8.6 all_gather.56
  39.2 7.8 all_gather.54
  47.0 8.6 all_gather.57
  80.7 27.6 %copy.75 = pred[384,384,32]{1,2,0:T(32,128)(4,1)} copy(pred[384,384,32]{0,2,1:T(32,128)(4,1)} %iota_compare_fusion) | data formatting | bytes 9437184 | tf_op jit(solution)/shard_map/eq | solution.py:18
  108.3 6.4 convolution_bitcast_fusion
  118.7 11.2 convolution_convert_fusion.1
  129.9 28.1 %fusion.186 = (f32[16,3,384]{2,1,0:T(4,128)S(1)}, f32[16,3,384,384]{2,3,1,0:T(8,128)}) fusion(bf16[16,3,384,384]{2,3,1,0:T(8,128)(2,1)} %convolution_convert_fusion.1, f32[3,384,384]{1,2,0:T(8,128)} %copy.76, pred[384,384]{0,1:T(8,128)(4,1)S(1)} %copy-done.47), kind=kOutput, calls=%fused_computation.205 | output fusion | flops 56623488 | bytes 44457984 | tf_op jit(solution)/shard_map/sub | solution.py:69
  158.0 13.5 fusion.124
  171.6 6.3 bitcast_convert_fusion.2
  177.9 7.1 all-gather.1
  185.1 8.6 all_gather.60
  193.7 7.8 all_gather.61
  201.5 8.6 all_gather.58
  210.1 7.8 all_gather.62
  222.4 103.1 %all-reduce.11.cloned.1.call-done = bf16[16,384,512]{2,1,0:T(8,128)(2,1)} async-done(((bf16[16,384,512]{2,1,0:T(8,128)(2,1)}), bf16[16,384,512]{2,1,0:T(8,128)(2,1)}) %all-reduce.11.cloned.1.call-update) | async-done | bytes 6291472 | tf_op jit(solution)/shard_map/psum | solution.py:104
  325.5 9.6 fusion.52
  355.3 7.9 all-gather.2
  363.3 10.1 all_gather.64
  373.4 10.2 all_gather.65
  383.5 9.4 all_gather.66
  393.7 8.5 convolution_convert_fusion.4
  402.3 100.5 %all-reduce.13.cloned.1.call-done = bf16[16,384,512]{2,1,0:T(8,128)(2,1)} async-done(((bf16[16,384,512]{2,1,0:T(8,128)(2,1)}), bf16[16,384,512]{2,1,0:T(8,128)(2,1)}) %all-reduce.13.cloned.1.call-update) | async-done | bytes 6291472 | tf_op jit(solution)/shard_map/psum | solution.py:104
  502.8 10.2 fusion.57
  513.8 7.6 convolution_convert_fusion.6
  522.8 15.6 fusion.43
  538.4 6.4 fusion.167
  544.8 11.8 add_convert_fusion
  556.7 147.5 %all-reduce.15.cloned.1.call-done = bf16[16,384,512]{2,1,0:T(8,128)(2,1)} async-done(((bf16[16,384,512]{2,1,0:T(8,128)(2,1)}), bf16[16,384,512]{2,1,0:T(8,128)(2,1)}) %all-reduce.15.cloned.1.call-update) | async-done | bytes 6291472 | tf_op jit(solution)/shard_map/psum | solution.py:104
  704.2 9.2 fusion.56
  713.4 7.3 fusion.38
  727.0 9.0 fusion.22
  736.1 6.5 fusion.24
  753.4 10.7 convolution_convert_fusion.5
  771.5 6.4 fusion.145
  781.8 119.1 %all-reduce.17.cloned.1.call-done = bf16[16,384,512]{2,1,0:T(8,128)(2,1)} async-done(((bf16[16,384,512]{2,1,0:T(8,128)(2,1)}), bf16[16,384,512]{2,1,0:T(8,128)(2,1)}) %all-reduce.17.cloned.1.call-update) | async-done | bytes 6291472 | tf_op jit(solution)/shard_map/psum | solution.py:104
  900.9 8.6 fusion.51
  909.5 7.6 fusion.35
  923.3 13.2 fusion.127
  936.5 18.0 %fusion.1 = (f32[16,3,384]{2,1,0:T(4,128)S(1)}, bf16[16,3,384,384]{2,3,1,0:T(8,128)(2,1)}) fusion(f32[16,3,384,384]{2,3,1,0:T(8,128)} %get-tuple-element.38, f32[16,3,384]{2,1,0:T(4,128)S(1)} %copy-done.49, bf16[16,384,3,64]{1,3,2,0:T(8,128)(2,1)} %copy-done.19, bf16[16,384,3,64]{1,3,2,0:T(8,128)(2,1)} %convolution_convert_fusion.13), kind=kOutput, calls=%fused_computation.3 | convolution fusion | flops 941340672 | bytes 47333376 | tf_op jit(solution)/shard_map/bqhe,bkhe->bhqk/dot_general | solution.py:75
  954.4 22.7 %fusion.17 = (bf16[3,384,384]{1,2,0:T(8,128)(2,1)}, bf16[16,3,384,384]{2,3,1,0:T(8,128)(2,1)}) fusion(bf16[16,3,384,384]{2,3,1,0:T(8,128)(2,1)} %get-tuple-element.46, f32[16,3,384]{2,1,0:T(4,128)S(1)} %get-tuple-element.45, f32[16,3,384,384]{2,3,1,0:T(8,128)} %get-tuple-element.38, f32[16,3,384]{2,1,0:T(4,128)S(1)} %copy-done.49), kind=kLoop, calls=%fused_computation.36 | loop fusion | flops 42024960 | bytes 57655296 | tf_op jit(solution)/shard_map/reduce_sum | solution.py:166
  977.2 12.3 convolution_convert_fusion.8
  989.4 8.2 convolution_convert_fusion.9
  997.7 6.3 fusion.101
  1004.1 6.3 fusion.105
  1010.4 12.8 fusion.64
  1023.9 9.2 fusion.153
  1033.2 12.1 fusion.156
  1045.4 12.7 convolution_bitcast_fusion.1
  1106.2 267.0 %all-reduce.19.cloned.1.call-done = (bf16[16,384,512]{2,1,0:T(8,128)(2,1)}, bf16[16,384,512]{2,1,0:T(8,128)(2,1)}, bf16[16,192,512]{2,1,0:T(8,128)(2,1)}) async-done(((bf16[16,384,512]{2,1,0:T(8,128)(2,1)}, bf16[16,384,512]{2,1,0:T(8,128)(2,1)}, bf16[16,192,512]{2,1,0:T(8,128)(2,1)}), (bf16[16,384,512]{2,1,0:T(8,128)(2,1)}, bf16[16,384,512]{2,1,0:T(8,128)(2,1)}, ...) | async-done | bytes 15728656 | tf_op jit(solution)/shard_map/psum | solution.py:104
  1373.2 8.4 fusion.46
  1381.7 14.8 fusion.32
  1396.6 7.0 all-reduce.3
  1405.3 12.2 reduce-scatter.30.cloned.1.call-done
  1417.5 22.2 %reduce-scatter.32.cloned.1.call-done = f32[512,128]{1,0:T(8,128)} async-done(((f32[512,512]{1,0:T(8,128)}), f32[512,128]{1,0:T(8,128)}) %reduce-scatter.32.cloned.1.call-update) | async-done | bytes 262160 | tf_op jit(solution)/shard_map/reduce_scatter | solution.py:108
  1439.7 18.2 %reduce-scatter.26.cloned.1.call-done = f32[192,128]{1,0:T(8,128)} async-done(((f32[192,512]{1,0:T(8,128)}), f32[192,128]{1,0:T(8,128)}) %reduce-scatter.26.cloned.1.call-update) | async-done | bytes 98320 | tf_op jit(solution)/shard_map/reduce_scatter | solution.py:108
  1458.0 18.1 %reduce-scatter.24.cloned.1.call-done = f32[128,192]{0,1:T(8,128)} async-done(((f32[512,192]{0,1:T(8,128)}), f32[128,192]{0,1:T(8,128)}) %reduce-scatter.24.cloned.1.call-update) | async-done | bytes 98320 | tf_op jit(solution)/shard_map/reduce_scatter | solution.py:108
  1476.0 18.2 %reduce-scatter.20.cloned.1.call-done = f32[128,192]{0,1:T(8,128)} async-done(((f32[512,192]{0,1:T(8,128)}), f32[128,192]{0,1:T(8,128)}) %reduce-scatter.20.cloned.1.call-update) | async-done | bytes 98320 | tf_op jit(solution)/shard_map/reduce_scatter | solution.py:108
  1494.3 18.1 %reduce-scatter.22.cloned.1.call-done = f32[128,192]{0,1:T(8,128)} async-done(((f32[512,192]{0,1:T(8,128)}), f32[128,192]{0,1:T(8,128)}) %reduce-scatter.22.cloned.1.call-update) | async-done | bytes 98320 | tf_op jit(solution)/shard_map/reduce_scatter | solution.py:108
  1512.3 18.2 %reduce-scatter.18.cloned.1.call-done = f32[192,128]{1,0:T(8,128)} async-done(((f32[192,512]{1,0:T(8,128)}), f32[192,128]{1,0:T(8,128)}) %reduce-scatter.18.cloned.1.call-update) | async-done | bytes 98320 | tf_op jit(solution)/shard_map/reduce_scatter | solution.py:108
  1530.5 18.1 %reduce-scatter.16.cloned.1.call-done = f32[128,192]{0,1:T(8,128)} async-done(((f32[512,192]{0,1:T(8,128)}), f32[128,192]{0,1:T(8,128)}) %reduce-scatter.16.cloned.1.call-update) | async-done | bytes 98320 | tf_op jit(solution)/shard_map/reduce_scatter | solution.py:108
  1548.6 18.1 %reduce-scatter.12.cloned.1.call-done = f32[128,192]{0,1:T(8,128)} async-done(((f32[512,192]{0,1:T(8,128)}), f32[128,192]{0,1:T(8,128)}) %reduce-scatter.12.cloned.1.call-update) | async-done | bytes 98320 | tf_op jit(solution)/shard_map/reduce_scatter | solution.py:108
  1566.7 18.1 %reduce-scatter.14.cloned.1.call-done = f32[128,192]{0,1:T(8,128)} async-done(((f32[512,192]{0,1:T(8,128)}), f32[128,192]{0,1:T(8,128)}) %reduce-scatter.14.cloned.1.call-update) | async-done | bytes 98320 | tf_op jit(solution)/shard_map/reduce_scatter | solution.py:108
  (249 shorter events, 150.2 us)
Async XLA Ops:
  7.2 210.8 %copy-start = (bf16[16,192,512]{2,1,0:T(8,128)(2,1)S(1)}, bf16[16,192,512]{2,1,0:T(8,128)(2,1)}, u32[]{:S(2)}) copy-start(bf16[16,192,512]{2,1,0:T(8,128)(2,1)} %param.20) | copy-start | bytes 9437188
  7.2 48.4 %copy-start.68 = (s32[15]{0:T(128)S(1)}, s32[15]{0:T(128)}, u32[]{:S(2)}) copy-start(s32[15]{0:T(128)} %constant.39.clone) | copy-start | bytes 184
  7.2 15.5 copy-start.50
  7.2 23.3 %copy-start.51 = (bf16[128,192]{0,1:T(8,128)(2,1)S(1)}, bf16[128,192]{0,1:T(8,128)(2,1)}, u32[]{:S(2)}) copy-start(bf16[128,192]{0,1:T(8,128)(2,1)} %param.24) | copy-start | bytes 147460
  7.2 318.3 %all-reduce.11.cloned.1.call-start = ((), (), s32[]{:S(2)}) async-start(), calls=%async_computation.11 | async-start | bytes 12582912 | tf_op jit(solution)/shard_map/psum | solution.py:104
  7.3 31.9 %copy-start.52 = (bf16[128,192]{0,1:T(8,128)(2,1)S(1)}, bf16[128,192]{0,1:T(8,128)(2,1)}, u32[]{:S(2)}) copy-start(bf16[128,192]{0,1:T(8,128)(2,1)} %param.25) | copy-start | bytes 147460
  7.3 39.7 %copy-start.53 = (bf16[192,128]{1,0:T(8,128)(2,1)S(1)}, bf16[192,128]{1,0:T(8,128)(2,1)}, u32[]{:S(2)}) copy-start(bf16[192,128]{1,0:T(8,128)(2,1)} %param.26) | copy-start | bytes 147460
  18.0 53.8 %copy-start.58 = (f32[4,1,128]{2,1,0:T(1,128)}, f32[4,1,128]{2,1,0:T(1,128)S(1)}, u32[]{:S(2)}) copy-start(f32[4,1,128]{2,1,0:T(1,128)S(1)} %convert_element_type.319) | copy-start | bytes 6148
  30.6 41.2 %copy-start.24 = (bf16[512,192]{0,1:T(8,128)(2,1)}, bf16[512,192]{0,1:T(8,128)(2,1)S(1)}, u32[]{:S(2)}) copy-start(bf16[512,192]{0,1:T(8,128)(2,1)S(1)} %all_gather.55) | copy-start | bytes 589828
  47.0 18.6 %copy-start.26 = (bf16[512,192]{0,1:T(8,128)(2,1)}, bf16[512,192]{0,1:T(8,128)(2,1)S(1)}, u32[]{:S(2)}) copy-start(bf16[512,192]{0,1:T(8,128)(2,1)S(1)} %all_gather.54) | copy-start | bytes 589828
  59.6 12.2 slice-start
  75.9 32.5 %copy-start.67 = (bf16[32,3]{0,1:T(4,128)(2,1)S(1)}, bf16[32,3]{0,1:T(4,128)(2,1)}, u32[]{:S(2)}) copy-start(bf16[32,3]{0,1:T(4,128)(2,1)} %param.22) | copy-start | bytes 580
  118.7 11.2 copy-start.47
  158.0 13.5 copy-start.48
  158.0 13.5 copy-start.30
  171.5 13.5 copy-start.54
  171.5 22.1 %copy-start.55 = (bf16[128,192]{0,1:T(8,128)(2,1)S(1)}, bf16[128,192]{0,1:T(8,128)(2,1)}, u32[]{:S(2)}) copy-start(bf16[128,192]{0,1:T(8,128)(2,1)} %param.28) | copy-start | bytes 147460
  171.6 29.9 %copy-start.56 = (bf16[128,192]{0,1:T(8,128)(2,1)S(1)}, bf16[128,192]{0,1:T(8,128)(2,1)}, u32[]{:S(2)}) copy-start(bf16[128,192]{0,1:T(8,128)(2,1)} %param.29) | copy-start | bytes 147460
  171.6 38.5 %copy-start.57 = (bf16[192,128]{1,0:T(8,128)(2,1)S(1)}, bf16[192,128]{1,0:T(8,128)(2,1)}, u32[]{:S(2)}) copy-start(bf16[192,128]{1,0:T(8,128)(2,1)} %param.30) | copy-start | bytes 147460
  177.9 324.9 %all-reduce.13.cloned.1.call-start = ((), (), s32[]{:S(2)}) async-start(), calls=%async_computation.12 | async-start | bytes 12582912 | tf_op jit(solution)/shard_map/psum | solution.py:104
  185.1 150.1 %copy-start.60 = (f32[4,1,128]{2,1,0:T(1,128)}, f32[4,1,128]{2,1,0:T(1,128)S(1)}, u32[]{:S(2)}) copy-start(f32[4,1,128]{2,1,0:T(1,128)S(1)} %convert_element_type.320) | copy-start | bytes 6148
  201.5 18.7 %copy-start.34 = (bf16[512,192]{0,1:T(8,128)(2,1)}, bf16[512,192]{0,1:T(8,128)(2,1)S(1)}, u32[]{:S(2)}) copy-start(bf16[512,192]{0,1:T(8,128)(2,1)S(1)} %all_gather.61) | copy-start | bytes 589828
  210.1 7.9 copy-start.32
  342.8 6.5 copy-start.5
  355.3 348.9 %all-reduce.15.cloned.1.call-start = ((), (), s32[]{:S(2)}) async-start(), calls=%async_computation.13 | async-start | bytes 12582912 | tf_op jit(solution)/shard_map/psum | solution.py:104
  363.3 350.1 %copy-start.63 = (f32[4,1,128]{2,1,0:T(1,128)}, f32[4,1,128]{2,1,0:T(1,128)S(1)}, u32[]{:S(2)}) copy-start(f32[4,1,128]{2,1,0:T(1,128)S(1)} %convert_element_type.321) | copy-start | bytes 6148
  513.7 7.6 copy-start.43
  513.7 7.6 copy-start.1
  513.7 7.6 copy-start.22
  513.7 9.0 copy-start.75
  556.6 344.3 %all-reduce.17.cloned.1.call-start = ((), (), s32[]{:S(2)}) async-start(), calls=%async_computation.14 | async-start | bytes 12582912 | tf_op jit(solution)/shard_map/psum | solution.py:104
  704.2 9.2 copy-start.7
  704.2 9.2 copy-start.44
  704.2 22.8 %slice-start.2 = ((s8[7077888]{0:T(1024)(128)(4,1)}), s8[4194304]{0:T(1024)(128)(4,1)S(1)}, s32[]{:S(2)}) async-start(s8[7077888]{0:T(1024)(128)(4,1)} %bitcast.271), calls=%async_computation.29 | async-start | bytes 8388608
  713.4 13.6 slice-start.3
  736.0 9.4 copy-start.12
  753.4 619.8 %all-reduce.19.cloned.1.call-start = ((), (), s32[]{:S(2)}) async-start(), calls=%async_computation.26 | async-start | bytes 31457280 | tf_op jit(solution)/shard_map/psum | solution.py:104
  753.4 10.8 copy-start.14
  764.2 7.3 copy-start.18
  770.4 7.4 copy-start.17
  771.5 7.6 copy-start.33
  779.1 121.8 %copy-start.41 = (f32[16,384]{1,0:T(8,128)S(1)}, f32[16,384]{1,0:T(8,128)}, u32[]{:S(2)}) copy-start(f32[16,384]{1,0:T(8,128)} %copy-done.40) | copy-start | bytes 73732
  779.1 121.8 %copy-start.61 = (f32[4,1,128]{2,1,0:T(1,128)S(1)}, f32[4,1,128]{2,1,0:T(1,128)}, u32[]{:S(2)}) copy-start(f32[4,1,128]{2,1,0:T(1,128)} %copy-done.60) | copy-start | bytes 6148
  900.9 8.6 copy-start.6
  909.5 10.2 copy-start.31
  989.4 8.2 copy-start.9
  989.4 8.2 copy-start.29
  1023.2 382.1 %reduce-scatter.28.cloned.1.call-start = ((), (), s32[]{:S(2)}) async-start(), calls=%async_computation.23 | async-start | bytes 1310720 | tf_op jit(solution)/shard_map/reduce_scatter | solution.py:108
  1033.1 384.4 %reduce-scatter.30.cloned.1.call-start = ((), (), s32[]{:S(2)}) async-start(), calls=%async_computation.24 | async-start | bytes 1310720 | tf_op jit(solution)/shard_map/reduce_scatter | solution.py:108
  1045.3 394.4 %reduce-scatter.32.cloned.1.call-start = ((), (), s32[]{:S(2)}) async-start(), calls=%async_computation.25 | async-start | bytes 1310720 | tf_op jit(solution)/shard_map/reduce_scatter | solution.py:108
  1058.2 399.8 %reduce-scatter.26.cloned.1.call-start = ((), (), s32[]{:S(2)}) async-start(), calls=%async_computation.22 | async-start | bytes 491520 | tf_op jit(solution)/shard_map/reduce_scatter | solution.py:108
  1063.9 412.1 %reduce-scatter.24.cloned.1.call-start = ((), (), s32[]{:S(2)}) async-start(), calls=%async_computation.21 | async-start | bytes 491520 | tf_op jit(solution)/shard_map/reduce_scatter | solution.py:108
  1067.0 6.6 copy-start.72
  1067.0 427.3 %reduce-scatter.20.cloned.1.call-start = ((), (), s32[]{:S(2)}) async-start(), calls=%async_computation.19 | async-start | bytes 491520 | tf_op jit(solution)/shard_map/reduce_scatter | solution.py:108
  1073.6 438.8 %reduce-scatter.22.cloned.1.call-start = ((), (), s32[]{:S(2)}) async-start(), calls=%async_computation.20 | async-start | bytes 491520 | tf_op jit(solution)/shard_map/reduce_scatter | solution.py:108
  1077.9 452.7 %reduce-scatter.18.cloned.1.call-start = ((), (), s32[]{:S(2)}) async-start(), calls=%async_computation.18 | async-start | bytes 491520 | tf_op jit(solution)/shard_map/reduce_scatter | solution.py:108
  1087.6 461.1 %reduce-scatter.16.cloned.1.call-start = ((), (), s32[]{:S(2)}) async-start(), calls=%async_computation.17 | async-start | bytes 491520 | tf_op jit(solution)/shard_map/reduce_scatter | solution.py:108
  1093.7 473.0 %reduce-scatter.12.cloned.1.call-start = ((), (), s32[]{:S(2)}) async-start(), calls=%async_computation.15 | async-start | bytes 491520 | tf_op jit(solution)/shard_map/reduce_scatter | solution.py:108
  1099.8 484.9 %reduce-scatter.14.cloned.1.call-start = ((), (), s32[]{:S(2)}) async-start(), calls=%async_computation.16 | async-start | bytes 491520 | tf_op jit(solution)/shard_map/reduce_scatter | solution.py:108
  1373.2 8.5 slice-start.4
  1373.2 8.5 copy-start.16
  1373.2 8.5 slice-start.5
  1381.7 14.9 copy-start.65
  1381.7 14.9 copy-start.66
  (34 other events, 143.7 us)
Sparse Core Ops, SparseCore 0:
  178.0 147.4 all-reduce.10
  355.4 147.3 all-reduce.12
  556.7 147.3 all-reduce.14
  753.5 147.3 all-reduce.16
  1023.3 349.8 all-reduce.18
  1376.1 19.1 reduce-scatter.27
  1398.3 19.1 reduce-scatter.29
  1420.6 19.1 reduce-scatter.31
  1442.8 15.1 reduce-scatter.25
  1460.9 15.1 reduce-scatter.23
  1479.1 15.1 reduce-scatter.19
  1497.1 15.1 reduce-scatter.21
  1515.4 15.1 reduce-scatter.17
  1533.4 15.1 reduce-scatter.15
  1551.5 15.1 reduce-scatter.11
  1569.6 15.1 reduce-scatter.13
where the time goes:
time: 1600 us
  waiting for transfers between devices  917 us (57%)
  matrix products  328 us (20%)
  other arithmetic  149 us (9%)
  blocking collectives  127 us (8%)
  local copies, waits for them, and re-layouts  56.4 us (4%)
    psum x5, waiting for transfers between devices, model_sum(): return lax.psum(partial.astype(jnp.bfloat16), 'model')  737 us
    reduce_scatter x11, waiting for transfers between devices, data_scatter(): lax.psum_scatter(grad_full, 'data', scatter_dimension=dim_idx, tiled=True)  179 us
    all_gather x6, blocking collectives, gather_data(): return lax.all_gather(w_shard, 'data', axis=dim_idx, tiled=True)  54.6 us
    all_gather x6, blocking collectives, gather_in(): w_full = lax.all_gather(w_shard, 'data', axis=0, tiled=True)  49.3 us
    dot_general x6, matrix products, back_in(): jnp.einsum('bshe,dhe->bsd', d_heads, weight, preferred_element_type=jnp.f...  33.6 us
  transfers between devices with their start and end apart: 16, of which 15 were waited for; matrix products, arithmetic and copies ran while one was open for 9% of the time, Pallas kernels for 0%

commit v1 on v0

v1 whole, which is shorter than its diff:
```python
import functools
import math
import jax
import jax.numpy as jnp
from jax import lax
from jax.experimental import pallas as pl
from jax.experimental.pallas import tpu as pltpu
from jax.sharding import PartitionSpec as P

EPS = 1e-6
BUCKET_EDGES = tuple(math.ceil(16 * 8.0 ** (bucket_no / 16.0)) for bucket_no in range(1, 16))
NUM_BUCKETS = 32
D, INNER, FF = 512, 384, 1024
T, E = 384, 192
PAIRS, BLK = 3, 128
ROW_OFF = (0, 128, 384)
F32, BF = jnp.float32, jnp.bfloat16
GELU_C = math.sqrt(2.0 / math.pi)
VMEM_LIMIT = 60 * 1024 * 1024


def nn(lhs, rhs):
    return lax.dot_general(lhs, rhs, (((1,), (0,)), ((), ())), preferred_element_type=F32)


def nt(lhs, rhs):
    return lax.dot_general(lhs, rhs, (((1,), (1,)), ((), ())), preferred_element_type=F32)


def tn(lhs, rhs):
    return lax.dot_general(lhs, rhs, (((0,), (0,)), ((), ())), preferred_element_type=F32)


def bf(val):
    return val.astype(BF)


def rounded(val):
    return val.astype(BF).astype(F32)


def unit_norm(act):
    act_f = act.astype(F32)
    inv_rms = lax.rsqrt(jnp.mean(act_f * act_f, axis=-1, keepdims=True) + EPS)
    return act_f * inv_rms, inv_rms


def norm_back(d_norm, unit_act, inv_rms, gain):
    d_norm_f = rounded(d_norm)
    d_unit = d_norm_f * gain
    d_act = inv_rms * (d_unit - unit_act * jnp.mean(d_unit * unit_act, axis=-1, keepdims=True))
    return d_act, jnp.sum(d_norm_f * unit_act, axis=0, keepdims=True)


def half_masks():
    lane = lax.broadcasted_iota(jnp.int32, (1, BLK), 1)
    low = jnp.where(lane < 64, 1.0, 0.0)
    return bf(low), bf(1.0 - low), lane < 64


def pick_half(low_rows, high_rows):
    lane = lax.broadcasted_iota(jnp.int32, low_rows.shape, 1)
    return jnp.where(lane < 64, low_rows, high_rows)


def unpack_weights(pack_ref, w_ref):
    for row in range(4):
        for mat in range(4):
            parts = [pack_ref[4 * half + row, :, mat * 192:(mat + 1) * 192] for half in range(2)]
            w_ref[row * BLK:(row + 1) * BLK, mat * INNER:(mat + 1) * INNER] = jnp.concatenate(parts, axis=1)


def pack_grads(acc_ref, out_ref):
    for row in range(4):
        for half in range(2):
            parts = [acc_ref[row * BLK:(row + 1) * BLK, mat * INNER + half * 192:mat * INNER + half * 192 + 192] for mat in range(4)]
            out_ref[4 * half + row] = jnp.concatenate(parts, axis=1)


def bucket_block(diag):
    row = lax.broadcasted_iota(jnp.int32, (BLK, BLK), 0)
    col = lax.broadcasted_iota(jnp.int32, (BLK, BLK), 1)
    rel = row - col + diag * BLK
    bucket = jnp.clip(rel, 0, 16)
    for edge in BUCKET_EDGES:
        bucket = bucket + jnp.where(rel >= edge, 1, 0)
    return rel, bucket


def build_bias(table_ref, bias_ref):
    for diag in range(3):
        rel, bucket = bucket_block(diag)
        for head in range(6):
            row = jnp.broadcast_to(table_ref[head:head + 1, :], (BLK, BLK))
            vals = jnp.take_along_axis(row, bucket, axis=1, mode="promise_in_bounds")
            bias_ref[head, diag] = jnp.where(rel >= 0, vals, -jnp.inf)


def self_fwd(part_ref, pack_ref, gain_ref, table_ref, x_ref, x1_ref, qkv_ref, p_ref, ctx_ref, w_ref, bias_ref):
    @pl.when(pl.program_id(0) == 0)
    def _():
        unpack_weights(pack_ref, w_ref)
        build_bias(table_ref, bias_ref)

    low, high, _ = half_masks()
    x_in = x_ref[0]
    unit_act, _ = unit_norm(x_in)
    normed = bf(unit_act * gain_ref[0:1, :])
    qkv_ref[0] = bf(nn(normed, w_ref[:, :3 * INNER]))
    for pair in range(PAIRS):
        lanes = pl.ds(pair * BLK, BLK)
        q_pair = qkv_ref[0, :, pl.ds(pair * BLK, BLK)]
        k_pair = qkv_ref[0, :, pl.ds(INNER + pair * BLK, BLK)]
        v_pair = qkv_ref[0, :, pl.ds(2 * INNER + pair * BLK, BLK)]
        k_heads = (k_pair * low, k_pair * high)
        v_heads = (v_pair * low, v_pair * high)
        for blk in range(3):
            keys = (blk + 1) * BLK
            q_rows = q_pair[blk * BLK:(blk + 1) * BLK]
            probs = []
            for sub in range(2):
                head = 2 * pair + sub
                bias = jnp.concatenate([bias_ref[head, blk - key_blk] for key_blk in range(blk + 1)], axis=1)
                logits = rounded(nt(q_rows, k_heads[sub][:keys])) + bias
                expd = jnp.exp(logits - jnp.max(logits, axis=1, keepdims=True))
                prob = expd * (1.0 / jnp.sum(expd, axis=1, keepdims=True))
                p_ref[0, head, :, ROW_OFF[blk]:ROW_OFF[blk] + keys] = prob
                probs.append(bf(prob))
            context = nn(jnp.concatenate(probs, axis=1), jnp.concatenate([v_heads[0][:keys], v_heads[1][:keys]], axis=0))
            ctx_ref[0, blk * BLK:(blk + 1) * BLK, lanes] = bf(context)
    x1_ref[0] = bf(x_in.astype(F32) + nt(ctx_ref[0], w_ref[:, 3 * INNER:]))


def cross_mlp(part_ref, pack_ref, mlp_ref, gain_ref, x1_ref, enc_ref, dy_ref,
              y_ref, dmid_ref, q_ref, kv_ref, p_ref, ctx_ref, dmlp_ref, dgain_ref,
              w_ref, hid_ref, dpre_ref):
    @pl.when(pl.program_id(0) == 0)
    def _():
        unpack_weights(pack_ref, w_ref)
        dmlp_ref[...] = jnp.zeros_like(dmlp_ref)
        dgain_ref[...] = jnp.zeros_like(dgain_ref)

    low, high, _ = half_masks()
    unit_act, _ = unit_norm(x1_ref[0])
    normed = bf(unit_act * gain_ref[1:2, :])
    q_ref[0] = bf(nn(normed, w_ref[:, :INNER]))
    kv_ref[0] = bf(nn(enc_ref[0], w_ref[:, INNER:3 * INNER]))
    for pair in range(PAIRS):
        lanes = pl.ds(pair * BLK, BLK)
        q_pair = q_ref[0, :, lanes]
        k_pair = kv_ref[0, :, lanes]
        v_pair = kv_ref[0, :, pl.ds(INNER + pair * BLK, BLK)]
        k_heads = (k_pair * low, k_pair * high)
        probs = []
        for sub in range(2):
            logits = rounded(nt(k_heads[sub], q_pair))
            expd = jnp.exp(logits - jnp.max(logits, axis=0, keepdims=True))
            prob = expd * (1.0 / jnp.sum(expd, axis=0, keepdims=True))
            p_ref[0, 2 * pair + sub] = prob
            probs.append(bf(prob))
        context = tn(jnp.concatenate(probs, axis=0), jnp.concatenate([v_pair * low, v_pair * high], axis=0))
        ctx_ref[0, :, lanes] = bf(context)
    mid_2 = rounded(x1_ref[0].astype(F32) + nt(ctx_ref[0], w_ref[:, 3 * INNER:]))

    unit_3, inv_3 = unit_norm(mid_2)
    gain_3 = gain_ref[2:3, :]
    normed_3 = bf(unit_3 * gain_3)
    dy = dy_ref[0]
    out = mid_2
    d_norm = jnp.zeros((T, D), F32)
    for half in range(2):
        wi_0 = mlp_ref[half, :, 0:512]
        wi_1 = mlp_ref[half, :, 512:1024]
        wo_t = mlp_ref[half, :, 1024:1536]
        pre_0 = rounded(nn(normed_3, wi_0))
        pre_1 = rounded(nn(normed_3, wi_1))
        d_hid = rounded(nn(dy, wo_t))
        sq = pre_0 * pre_0
        tanh = jnp.tanh(GELU_C * (pre_0 + 0.044715 * (sq * pre_0)))
        cdf = 0.5 * (1.0 + tanh)
        gelu = pre_0 * cdf
        slope = cdf + (0.5 * pre_0) * (1.0 - tanh * tanh) * (GELU_C * (1.0 + (3.0 * 0.044715) * sq))
        hid_ref[...] = bf(gelu * pre_1)
        dpre_ref[:, 0:512] = bf((d_hid * pre_1) * slope)
        dpre_ref[:, 512:1024] = bf(d_hid * gelu)
        out = out + nt(hid_ref[...], wo_t)
        d_norm = d_norm + nt(dpre_ref[...], mlp_ref[half, :, 0:1024])
        dmlp_ref[half, :, 0:1024] += tn(normed_3, dpre_ref[...])
        dmlp_ref[half, :, 1024:1536] += tn(dy, hid_ref[...])
    y_ref[0] = bf(out)
    d_act, d_gain = norm_back(d_norm, unit_3, inv_3, gain_3)
    dgain_ref[...] += jnp.broadcast_to(d_gain, (8, D))
    dmid_ref[0] = bf(dy.astype(F32) + d_act)


def cross_bwd(part_ref, pack_ref, gain_ref, x1_ref, enc_ref, dmid_ref, q_ref, kv_ref, p_ref, ctx_ref,
              dx1_ref, denc_ref, dw_ref, dgain_ref, w_ref, acc_ref, dq_ref, dkv_ref, dctx_ref):
    step = pl.program_id(0)

    @pl.when(step == 0)
    def _():
        unpack_weights(pack_ref, w_ref)
        acc_ref[...] = jnp.zeros_like(acc_ref)
        dgain_ref[...] = jnp.zeros_like(dgain_ref)

    low, high, _ = half_masks()
    d_mid = dmid_ref[0]
    dctx_ref[...] = bf(nn(d_mid, w_ref[:, 3 * INNER:]))
    acc_ref[:, 3 * INNER:] += tn(d_mid, ctx_ref[0])
    for pair in range(PAIRS):
        lanes = pl.ds(pair * BLK, BLK)
        q_pair = q_ref[0, :, lanes]
        k_pair = kv_ref[0, :, lanes]
        v_pair = kv_ref[0, :, pl.ds(INNER + pair * BLK, BLK)]
        dctx_pair = dctx_ref[:, lanes]
        v_heads = (v_pair * low, v_pair * high)
        probs, d_logits = [], []
        for sub in range(2):
            prob = p_ref[0, 2 * pair + sub]
            d_prob = rounded(nt(v_heads[sub], dctx_pair))
            delta = jnp.sum(prob * d_prob, axis=0, keepdims=True)
            d_logits.append(bf(prob * (d_prob - delta)))
            probs.append(bf(prob))
        d_logit = jnp.concatenate(d_logits, axis=0)
        dq_ref[:, lanes] = bf(tn(d_logit, jnp.concatenate([k_pair * low, k_pair * high], axis=0)))
        dk_both = nn(d_logit, q_pair)
        dkv_ref[:, lanes] = bf(pick_half(dk_both[:E], dk_both[E:]))
        dv_both = nn(jnp.concatenate(probs, axis=0), dctx_pair)
        dkv_ref[:, pl.ds(INNER + pair * BLK, BLK)] = bf(pick_half(dv_both[:E], dv_both[E:]))
    denc_ref[0] = bf(nt(dkv_ref[...], w_ref[:, INNER:3 * INNER]))
    acc_ref[:, INNER:3 * INNER] += tn(enc_ref[0], dkv_ref[...])
    unit_act, inv_rms = unit_norm(x1_ref[0])
    gain = gain_ref[1:2, :]
    acc_ref[:, :INNER] += tn(bf(unit_act * gain), dq_ref[...])
    d_act, d_gain = norm_back(nt(dq_ref[...], w_ref[:, :INNER]), unit_act, inv_rms, gain)
    dgain_ref[...] += jnp.broadcast_to(d_gain, (8, D))
    dx1_ref[0] = bf(d_mid.astype(F32) + d_act)

    @pl.when(step == pl.num_programs(0) - 1)
    def _():
        pack_grads(acc_ref, dw_ref)


def self_bwd(part_ref, pack_ref, gain_ref, x_ref, dmid_ref, qkv_ref, p_ref, ctx_ref,
             dx_ref, dw_ref, dgain_ref, dbias_ref, w_ref, acc_ref, dqkv_ref, dctx_ref):
    step = pl.program_id(0)

    @pl.when(step == 0)
    def _():
        unpack_weights(pack_ref, w_ref)
        acc_ref[...] = jnp.zeros_like(acc_ref)
        dgain_ref[...] = jnp.zeros_like(dgain_ref)
        dbias_ref[...] = jnp.zeros_like(dbias_ref)

    low, high, _ = half_masks()
    d_mid = dmid_ref[0]
    dctx_ref[...] = bf(nn(d_mid, w_ref[:, 3 * INNER:]))
    acc_ref[:, 3 * INNER:] += tn(d_mid, ctx_ref[0])
    for pair in range(PAIRS):
        q_pair = qkv_ref[0, :, pl.ds(pair * BLK, BLK)]
        k_pair = qkv_ref[0, :, pl.ds(INNER + pair * BLK, BLK)]
        v_pair = qkv_ref[0, :, pl.ds(2 * INNER + pair * BLK, BLK)]
        dctx_pair = dctx_ref[:, pl.ds(pair * BLK, BLK)]
        k_heads = (k_pair * low, k_pair * high)
        v_heads = (v_pair * low, v_pair * high)
        probs, d_logits = [[], []], [[], []]
        for blk in range(3):
            keys = (blk + 1) * BLK
            for sub in range(2):
                head = 2 * pair + sub
                prob = p_ref[0, head, :, ROW_OFF[blk]:ROW_OFF[blk] + keys]
                d_prob = rounded(nt(dctx_pair[blk * BLK:(blk + 1) * BLK], v_heads[sub][:keys]))
                delta = jnp.sum(prob * d_prob, axis=1, keepdims=True)
                d_logit = prob * (d_prob - delta)
                for key_blk in range(blk + 1):
                    dbias_ref[head, blk - key_blk] += d_logit[:, key_blk * BLK:(key_blk + 1) * BLK]
                d_logits[sub].append(bf(d_logit))
                probs[sub].append(bf(prob))
            d_query = nn(jnp.concatenate([d_logits[0][blk], d_logits[1][blk]], axis=1),
                         jnp.concatenate([k_heads[0][:keys], k_heads[1][:keys]], axis=0))
            dqkv_ref[blk * BLK:(blk + 1) * BLK, pl.ds(pair * BLK, BLK)] = bf(d_query)
        for vals, rhs, base in ((d_logits, q_pair, INNER), (probs, dctx_pair, 2 * INNER)):
            for key_blk in range(3):
                cols = slice(key_blk * BLK, (key_blk + 1) * BLK)
                left = jnp.concatenate([jnp.concatenate([vals[sub][blk][:, cols] for blk in range(key_blk, 3)], axis=0) for sub in range(2)], axis=1)
                both = tn(left, rhs[key_blk * BLK:])
                dqkv_ref[cols, pl.ds(base + pair * BLK, BLK)] = bf(pick_half(both[:BLK], both[BLK:]))
    unit_act, inv_rms = unit_norm(x_ref[0])
    gain = gain_ref[0:1, :]
    acc_ref[:, :3 * INNER] += tn(bf(unit_act * gain), dqkv_ref[...])
    d_act, d_gain = norm_back(nt(dqkv_ref[...], w_ref[:, :3 * INNER]), unit_act, inv_rms, gain)
    dgain_ref[...] += jnp.broadcast_to(d_gain, (8, D))
    dx_ref[0] = bf(d_mid.astype(F32) + d_act)

    @pl.when(step == pl.num_programs(0) - 1)
    def _():
        pack_grads(acc_ref, dw_ref)


def bucket_sums(dbias_ref, dg1_ref, dg2_ref, dg3_ref, out_ref):
    blocks = [bucket_block(diag) for diag in range(3)]
    buckets = [jnp.where(rel >= 0, bucket, -1) for rel, bucket in blocks]

    lane = lax.broadcasted_iota(jnp.int32, (8, BLK), 1)

    def one_bucket(bucket_no, sums):
        rows = []
        for head in range(6):
            total = jnp.zeros((BLK, BLK), F32)
            for diag in range(3):
                total = total + jnp.where(buckets[diag] == bucket_no, dbias_ref[head, diag], 0.0)
            rows.append(jnp.sum(total, axis=0, keepdims=True))
        rows += [jnp.zeros((1, BLK), F32)] * 2
        per_head = jnp.sum(jnp.concatenate(rows, axis=0), axis=1, keepdims=True)
        return jnp.where(lane == bucket_no, per_head, sums)

    out_ref[:, D:] = lax.fori_loop(0, NUM_BUCKETS, one_bucket, jnp.zeros((8, BLK), F32))
    row = lax.broadcasted_iota(jnp.int32, (8, D), 0)
    out_ref[:, :D] = jnp.where(row == 0, dg1_ref[...], jnp.where(row == 1, dg2_ref[...], dg3_ref[...]))


def seq_block(*dims):
    zeros = (0,) * len(dims)
    return pl.BlockSpec((1,) + dims, lambda i, part: (i,) + zeros)


def arg_block(*dims):
    zeros = (0,) * len(dims)
    return pl.BlockSpec((1,) + dims, lambda i, part: (part[0] * 8 + i,) + zeros)


def whole(*dims):
    zeros = (0,) * len(dims)
    return pl.BlockSpec(dims, lambda i, part: zeros)


def call(body, name, seqs, flops, in_specs, outs, scratch, *args):
    out_specs, out_shape = zip(*outs)
    return pl.pallas_call(
        body,
        name=name,
        out_shape=out_shape,
        grid_spec=pltpu.PrefetchScalarGridSpec(num_scalar_prefetch=1, grid=(seqs,), in_specs=in_specs, out_specs=out_specs, scratch_shapes=scratch),
        compiler_params=pltpu.CompilerParams(dimension_semantics=("arbitrary",), vmem_limit_bytes=VMEM_LIMIT),
        cost_estimate=pl.CostEstimate(flops=flops, bytes_accessed=40_000_000, transcendentals=0),
    )(*args)


def shape(dims, dtype):
    return jax.ShapeDtypeStruct(dims, dtype)


def seq_out(seqs, dims, dtype):
    return seq_block(*dims), shape((seqs,) + dims, dtype)


def whole_out(dims, dtype):
    return whole(*dims), shape(dims, dtype)


def layer_shard(dec_in, enc_out, grad_out, rel_bias, self_q, self_k, self_v, self_o, cross_q, cross_k, cross_v, cross_o, mlp_wi_0, mlp_wi_1, mlp_wo, norm_self, norm_cross, norm_mlp):
    axes = ("model", "data")
    seqs = dec_in.shape[0] // 2
    part = lax.axis_index("model").astype(jnp.int32).reshape(1)
    rows = (norm_self[None], norm_cross[None], norm_mlp[None], jnp.pad(rel_bias.T, ((0, 0), (0, BLK - NUM_BUCKETS))))
    small = sum(jnp.pad(val, ((pos, 16 - pos - val.shape[0]), (0, 0))) for pos, val in enumerate(rows))
    small = lax.all_gather(small, axes).astype(F32)
    gains = small[:4].transpose(1, 0, 2).reshape(16, D)[:8]
    table = small[:, 3:6].reshape(2, 4, 3, BLK)[:, 0].reshape(6, BLK)
    table = jnp.pad(table, ((0, 2), (0, 0)))
    w_self = lax.all_gather(jnp.concatenate([self_q, self_k, self_v, self_o.T], axis=1), axes)
    w_cross = lax.all_gather(jnp.concatenate([cross_q, cross_k, cross_v, cross_o.T], axis=1), axes)
    w_mlp = lax.all_gather(jnp.concatenate([mlp_wi_0, mlp_wi_1, mlp_wo.T], axis=1), axes).reshape(2, D, 1536)

    vmem = pltpu.VMEM
    pack_spec = whole(8, BLK, 768)
    w_scr = vmem((D, 1536), BF)
    acc_scr = vmem((D, 1536), F32)
    mid_1, qkv, probs, ctx = call(
        self_fwd, "self_fwd", seqs, 60_000_000_000,
        [pack_spec, whole(8, D), whole(8, BLK), arg_block(T, D)],
        [seq_out(seqs, (T, D), BF), seq_out(seqs, (T, 3 * INNER), BF), seq_out(seqs, (6, BLK, 768), F32), seq_out(seqs, (T, INNER), BF)],
        [w_scr, vmem((6, 3, BLK, BLK), F32)],
        part, w_self, gains, table, dec_in)
    dec_out, d_mid_2, q_x, kv_x, probs_x, ctx_x, d_mlp, d_gain_3 = call(
        cross_mlp, "cross_mlp", seqs, 120_000_000_000,
        [pack_spec, whole(2, D, 1536), whole(8, D), seq_block(T, D), arg_block(E, D), arg_block(T, D)],
        [seq_out(seqs, (T, D), BF), seq_out(seqs, (T, D), BF), seq_out(seqs, (T, INNER), BF), seq_out(seqs, (E, 2 * INNER), BF),
         seq_out(seqs, (6, E, T), F32), seq_out(seqs, (T, INNER), BF), whole_out((2, D, 1536), F32), whole_out((8, D), F32)],
        [w_scr, vmem((T, 512), BF), vmem((T, 1024), BF)],
        part, w_cross, w_mlp, gains, mid_1, enc_out, grad_out)
    dec_out = lax.all_gather(dec_out, "model", axis=0, tiled=True)
    d_mlp = lax.psum_scatter(d_mlp.reshape(8, BLK, 1536), axes, scatter_dimension=0)
    d_mid_1, grad_enc, d_cross, d_gain_2 = call(
        cross_bwd, "cross_bwd", seqs, 60_000_000_000,
        [pack_spec, whole(8, D), seq_block(T, D), arg_block(E, D), seq_block(T, D), seq_block(T, INNER), seq_block(E, 2 * INNER), seq_block(6, E, T), seq_block(T, INNER)],
        [seq_out(seqs, (T, D), BF), seq_out(seqs, (E, D), BF), whole_out((8, BLK, 768), F32), whole_out((8, D), F32)],
        [w_scr, acc_scr, vmem((T, INNER), BF), vmem((E, 2 * INNER), BF), vmem((T, INNER), BF)],
        part, w_cross, gains, mid_1, enc_out, d_mid_2, q_x, kv_x, probs_x, ctx_x)
    grad_enc = lax.all_gather(grad_enc, "model", axis=0, tiled=True)
    d_cross = lax.psum_scatter(d_cross, axes, scatter_dimension=0)
    grad_dec, d_self, d_gain_1, d_bias = call(
        self_bwd, "self_bwd", seqs, 90_000_000_000,
        [pack_spec, whole(8, D), arg_block(T, D), seq_block(T, D), seq_block(T, 3 * INNER), seq_block(6, BLK, 768), seq_block(T, INNER)],
        [seq_out(seqs, (T, D), BF), whole_out((8, BLK, 768), F32), whole_out((8, D), F32), whole_out((6, 3, BLK, BLK), F32)],
        [w_scr, acc_scr, vmem((T, 3 * INNER), BF), vmem((T, INNER), BF)],
        part, w_self, gains, dec_in, d_mid_1, qkv, probs, ctx)
    grad_dec = lax.all_gather(grad_dec, "model", axis=0, tiled=True)
    d_self = lax.psum_scatter(d_self, axes, scatter_dimension=0)
    tiny = pl.pallas_call(bucket_sums, name="bucket_sums", out_shape=shape((8, D + BLK), F32))(d_bias, d_gain_1, d_gain_2, d_gain_3)
    tiny = lax.psum(tiny, axes)
    data_no, model_no = lax.axis_index("data"), lax.axis_index("model")
    gain_grads = lax.dynamic_slice(tiny, (0, data_no * BLK), (3, BLK))
    gain_grads = (gain_grads[0], gain_grads[1], gain_grads[2])
    bias_sums = tiny[:, D:D + NUM_BUCKETS]
    grad_bias = jnp.where(model_no == 0, bias_sums[0:3], bias_sums[3:6]).T

    def split_attn(grad_pack):
        mats = [grad_pack[:, 192 * pos:192 * (pos + 1)] for pos in range(4)]
        return mats[0], mats[1], mats[2], mats[3].T

    return (dec_out, grad_dec, grad_enc, grad_bias) + split_attn(d_self) + split_attn(d_cross) + (
        d_mlp[:, 0:512], d_mlp[:, 512:1024], d_mlp[:, 1024:1536].T) + gain_grads


def solution(mesh):
    row_spec = P("data", None, None)
    col_in = P("data", "model")
    col_out = P("model", "data")
    gain_spec = P("data")
    bias_spec = P(None, "model")
    arg_specs = (row_spec, row_spec, row_spec, bias_spec, col_in, col_in, col_in, col_out, col_in, col_in, col_in, col_out, col_in, col_in, col_out, gain_spec, gain_spec, gain_spec)
    out_specs = (row_spec, row_spec, row_spec) + arg_specs[3:]
    return jax.shard_map(layer_shard, mesh=mesh, in_specs=arg_specs, out_specs=out_specs, check_vma=False)
```

time: 1600 us -> 565 us (0.35)
  waiting for transfers between devices: 917 us -> 272 us
  matrix products: 328 us -> 0 us
  Pallas kernels: 0 us -> 191 us
  other arithmetic: 149 us -> 6.11 us
  blocking collectives: 127 us -> 37 us
    psum x5 -> x0, waiting for transfers between devices: 737 us -> none  [model_sum(): return lax.psum(partial.astype(jnp.bfloat16), 'model')]
    dot_general x47 -> x0, matrix products: 328 us -> none  [the longest x6 33.6 us: back_in(): jnp.einsum('bshe,dhe->bsd', d_heads, weight, preferred_element_type=jnp.f...]
    pallas_call x0 -> x5, Pallas kernels: none -> 191 us  [the longest x4 183 us: call(): pl.pallas_call(body, name=name, out_shape=out_shape, grid_spec=pltpu.Pref...]
    all_gather x0 -> x6, waiting for transfers between devices: none -> 178 us  [the longest x1 79.8 us: layer_shard(): dec_out = lax.all_gather(dec_out, 'model', axis=0, tiled=True)]
    all_gather x14 -> x1, blocking collectives: 120 us -> 14 us  [layer_shard(): small = lax.all_gather(small, axes).astype(F32)]
    reduce_scatter x11 -> x3, waiting for transfers between devices: 179 us -> 91.5 us  [the longest x1 56.7 us: layer_shard(): lax.psum_scatter(d_mlp.reshape(8, BLK, 1536), axes, scatter_dimension=0)]
    reduce_sum x9 -> x0, other arithmetic: 76.7 us -> none  [the longest x3 26.2 us: norm_bwd(): return (d_act, jnp.sum(d_norm_f * unit_act, axis=(0, 1)))]
    convert_element_type x7 -> x1, other arithmetic: 36.3 us -> 0.01 us  [layer_shard(): small = lax.all_gather(small, axes).astype(F32)]
  transfers between devices with their start and end apart: 16 -> 9, of which waited for: 15 -> 6; matrix products, arithmetic and copies ran while one was open for 9% -> 5% of each run, Pallas kernels for 0% -> 17%
where the time goes in v1:
time: 565 us
  waiting for transfers between devices  272 us (48%)
  Pallas kernels  191 us (34%)
  local copies, waits for them, and re-layouts  44.2 us (8%)
  blocking collectives  37 us (7%)
  between operations  14 us (2%)
  other arithmetic  6.11 us (1%)
    pallas_call x4, Pallas kernels, call(): pl.pallas_call(body, name=name, out_shape=out_shape, grid_spec=pltpu.Pref...  183 us
    all_gather x1, waiting for transfers between devices, layer_shard(): dec_out = lax.all_gather(dec_out, 'model', axis=0, tiled=True)  79.8 us
    all_gather x1, waiting for transfers between devices, layer_shard(): grad_dec = lax.all_gather(grad_dec, 'model', axis=0, tiled=True)  75.5 us
    reduce_scatter x1, waiting for transfers between devices, layer_shard(): lax.psum_scatter(d_mlp.reshape(8, BLK, 1536), axes, scatter_dimension=0)  56.7 us
    reduce_scatter x1, waiting for transfers between devices, layer_shard(): d_cross = lax.psum_scatter(d_cross, axes, scatter_dimension=0)  34.8 us
    psum x1, blocking collectives, layer_shard(): tiny = lax.psum(tiny, axes)  23 us
    unnamed x22, local copies, waits for them, and re-layouts  21.7 us
    all_gather x1, waiting for transfers between devices, layer_shard(): lax.all_gather(jnp.concatenate([cross_q, cross_k, cross_v, cross_o.T], ax...  19.8 us
  transfers between devices with their start and end apart: 9, of which 6 were waited for; matrix products, arithmetic and copies ran while one was open for 5% of the time, Pallas kernels for 17%

profile of v1, /device:TPU:0, one launch (start us, length us, event | category | flops | bytes accessed | tf_op | source)
XLA Modules:
  0.0 564.6 jit_solution(13544726721018704634)
XLA Ops:
  7.2 0.0 all-gather.21.cloned.1.call-start
  7.2 1.6 pad_maximum_fusion.2
  8.8 0.0 all-gather.21.cloned.1.call-update
  8.8 0.0 all-gather.17.cloned.1.call-start
  8.9 1.6 pad_maximum_fusion.1
  10.4 0.0 all-gather.17.cloned.1.call-update
  10.5 0.0 all-gather.19.cloned.1.call-start
  10.5 1.0 copy.71
  11.5 1.0 copy.72
  12.6 1.7 pad_maximum_fusion
  14.3 0.0 all-gather.19.cloned.1.call-update
  14.3 0.0 all-gather.15.cloned.1.call-start
  14.3 0.7 pad_add_fusion
  15.0 14.0 %all-gather.2 = bf16[128,128]{1,0:T(8,128)(2,1)S(1)} all-gather(bf16[16,128]{1,0:T(8,128)(2,1)S(1)} %pad_add_fusion), channel_id=4, replica_groups=mesh['model'=2,'data'=4] {'model','data'}, dimensions={0}, use_global_device_ids=true | all-gather | bytes 36864 | tf_op jit(solution)/shard_map/all_gather | solution.py:367
  29.1 0.6 slice_bitcast_fusion.3.gain_ref
  29.8 0.6 pad.29.table_ref
  30.4 3.2 all-gather.21.cloned.1.call-done
  33.6 2.6 copy.74
  36.2 19.8 %all-gather.17.cloned.1.call-done = bf16[1024,768]{0,1:T(8,128)(2,1)} async-done(((bf16[128,768]{0,1:T(8,128)(2,1)}), bf16[1024,768]{0,1:T(8,128)(2,1)}) %all-gather.17.cloned.1.call-update) | async-done | bytes 1572880 | tf_op jit(solution)/shard_map/all_gather | solution.py:372
  56.0 2.6 copy.70
  58.6 38.6 %self_fwd.1 = (bf16[8,384,512]{2,1,0:T(8,128)(2,1)}, bf16[8,384,1152]{2,1,0:T(8,128)(2,1)}, f32[8,6,128,768]{3,2,1,0:T(8,128)}, bf16[8,384,384]{2,1,0:T(8,128)(2,1)}) custom-call(s32[1]{0:T(128)} %bitcast.part_ref, bf16[8,128,768]{2,1,0:T(8,128)(2,1)} %bitcast.42, f32[8,512]{1,0:T(8,128)} %slice_bitcast_fusion.3.gain_ref, f32[8,128]{1,0:T(8,128)} %pad.29.table_ref, ...), custom_call_target="tpu_custom_call" | custom-call | flops 60000002048 | bytes 40000000 | tf_op jit(solution)/shard_map/self_fwd/pallas_call | solution.py:339
  97.2 0.0 all-gather.19.cloned.1.call-done
  97.2 4.6 copy.73
  101.8 63.5 %cross_mlp.1 = (bf16[8,384,512]{2,1,0:T(8,128)(2,1)}, bf16[8,384,512]{2,1,0:T(8,128)(2,1)}, bf16[8,384,384]{2,1,0:T(8,128)(2,1)}, bf16[8,192,768]{2,1,0:T(8,128)...) custom-call(s32[1]{0:T(128)} %bitcast.part_ref, ...), custom_call_target="tpu_custom_call" | custom-call | flops 120000004096 | bytes 40000000 | tf_op jit(solution)/shard_map/cross_mlp/pallas_call | solution.py:339
  165.4 32.8 %cross_bwd.1 = (bf16[8,384,512]{2,1,0:T(8,128)(2,1)}, bf16[8,192,512]{2,1,0:T(8,128)(2,1)}, f32[8,128,768]{2,1,0:T(8,128)}, f32[8,512]{1,0:T(8,128)}) custom-call(s32[1]{0:T(128)} %bitcast.part_ref, bf16[8,128,768]{2,1,0:T(8,128)(2,1)} %bitcast.45, f32[8,512]{1,0:T(8,128)} %slice_bitcast_fusion.3.gain_ref, bf16[8,384,512]{2,1,0:T(8,128)(2,1)} %get-tuple-element.38.x1_ref, ...), custom_call_target="tpu_custom_call" | custom-call | flops 60000002048 | bytes 40000000 | tf_op jit(solution)/shard_map/cross_bwd/pallas_call | solution.py:339
  198.2 0.0 all-gather.15.cloned.1.call-update
  198.2 0.0 reduce-scatter.4.cloned.1.call-start
  198.3 48.5 %self_bwd.1 = (bf16[8,384,512]{2,1,0:T(8,128)(2,1)}, f32[8,128,768]{2,1,0:T(8,128)}, f32[8,512]{1,0:T(8,128)}, f32[6,3,128,128]{3,2,1,0:T(8,128)}) custom-call(s32[1]{0:T(128)} %bitcast.part_ref, bf16[8,128,768]{2,1,0:T(8,128)(2,1)} %bitcast.43, f32[8,512]{1,0:T(8,128)} %slice_bitcast_fusion.3.gain_ref, bf16[16,384,512]{2,1,0:T(8,128)(2,1)} %x_ref.3, ...), custom_call_target="tpu_custom_call" | custom-call | flops 89999998976 | bytes 40000000 | tf_op jit(solution)/shard_map/self_bwd/pallas_call | solution.py:339
  246.8 0.0 reduce-scatter.4.cloned.1.call-update
  246.8 0.0 reduce-scatter.6.cloned.1.call-start
  246.9 0.5 reduce-scatter.6.cloned.1.call-update
  247.4 0.0 all-gather.13.cloned.1.call-start
  247.4 0.7 all-gather.13.cloned.1.call-update
  248.1 0.0 all-gather.11.cloned.1.call-start
  248.2 0.7 all-gather.11.cloned.1.call-update
  248.9 0.0 reduce-scatter.8.cloned.1.call-start
  248.9 6.6 %copy.77 = f32[8,128,1536]{1,2,0:T(8,128)} copy(f32[8,128,1536]{2,1,0:T(8,128)} %bitcast.40) | data formatting | bytes 12582912 | tf_op jit(solution)/shard_map/reshape | solution.py:393
  255.5 0.0 reduce-scatter.8.cloned.1.call-update
  255.5 7.6 %bucket_sums.1 = f32[8,640]{1,0:T(8,128)} custom-call(f32[6,3,128,128]{3,2,1,0:T(8,128)} %get-tuple-element.51.dbias_ref, f32[8,512]{1,0:T(8,128)} %get-tuple-element.52.dg1_ref, f32[8,512]{1,0:T(8,128)} %get-tuple-element.53.dg2_ref, f32[8,512]{1,0:T(8,128)} %get-tuple-element.54.dg3_ref), custom_call_target="tpu_custom_call" | custom-call | tf_op jit(solution)/shard_map/bucket_sums/pallas_call | solution.py:410
  263.1 23.0 %psum.7 = f32[8,640]{1,0:T(8,128)S(1)} all-reduce(f32[8,640]{1,0:T(8,128)} %bucket_sums.1), channel_id=1, replica_groups=mesh['model'=2,'data'=4] {'model','data'}, use_global_device_ids=true, to_apply=%region_0.1 | all-reduce | flops 5120 | bytes 40960 | tf_op jit(solution)/shard_map/psum | solution.py:411
  286.1 0.5 slice_bitcast_fusion.4
  286.6 0.6 fusion
  287.2 1.3 slice_bitcast_fusion.2
  288.4 0.7 copy.78
  289.2 0.7 copy.79
  289.9 0.7 copy.80
  290.7 0.7 copy.81
  291.4 34.8 %reduce-scatter.6.cloned.1.call-done = f32[1,128,768]{2,1,0:T(8,128)} async-done(((f32[8,128,768]{2,1,0:T(8,128)}), f32[1,128,768]{2,1,0:T(8,128)}) %reduce-scatter.6.cloned.1.call-update) | async-done | bytes 393232 | tf_op jit(solution)/shard_map/reduce_scatter | solution.py:401
  326.2 1.3 slice_bitcast_fusion.1
  327.5 0.7 copy.82
  328.2 0.7 copy.83
  329.0 0.7 copy.84
  329.7 0.7 copy.85
  330.5 75.5 %all-gather.13.cloned.1.call-done = bf16[16,384,512]{2,1,0:T(8,128)(2,1)} async-done(((bf16[8,384,512]{2,1,0:T(8,128)(2,1)}), bf16[16,384,512]{2,1,0:T(8,128)(2,1)}) %all-gather.13.cloned.1.call-update) | async-done | bytes 6291472 | tf_op jit(solution)/shard_map/all_gather | solution.py:408
  406.0 79.8 %all-gather.11.cloned.1.call-done = bf16[16,384,512]{2,1,0:T(8,128)(2,1)} async-done(((bf16[8,384,512]{2,1,0:T(8,128)(2,1)}), bf16[16,384,512]{2,1,0:T(8,128)(2,1)}) %all-gather.11.cloned.1.call-update) | async-done | bytes 6291472 | tf_op jit(solution)/shard_map/all_gather | solution.py:392
  485.8 56.7 %reduce-scatter.8.cloned.1.call-done = f32[1,128,1536]{1,2,0:T(8,128)} async-done(((f32[8,128,1536]{1,2,0:T(8,128)}), f32[1,128,1536]{1,2,0:T(8,128)}) %reduce-scatter.8.cloned.1.call-update) | async-done | bytes 786448 | tf_op jit(solution)/shard_map/reduce_scatter | solution.py:393
  542.5 1.9 slice_bitcast_fusion
  544.3 0.8 copy.86
  545.2 0.8 copy.87
  546.0 6.2 %copy.92 = bf16[16,384,512]{2,1,0:T(8,128)(2,1)} copy(bf16[16,384,512]{2,1,0:T(8,128)(2,1)} %all-gather.11.cloned.1.call-done) | data formatting | bytes 12582912
  552.2 0.0 slice-done
  552.2 3.2 copy.93
  555.4 1.0 copy-done
  556.4 1.7 copy.94
  (15 shorter events, 0.1 us)
Async XLA Ops:
  7.2 26.4 %all-gather.21.cloned.1.call-start = ((), (), s32[]{:S(2)}) async-start(), calls=%async_computation.11 | async-start | bytes 1769472 | tf_op jit(solution)/shard_map/all_gather | solution.py:371
  8.8 47.1 %all-gather.17.cloned.1.call-start = ((), (), s32[]{:S(2)}) async-start(), calls=%async_computation.9 | async-start | bytes 1769472 | tf_op jit(solution)/shard_map/all_gather | solution.py:372
  10.5 86.7 %all-gather.19.cloned.1.call-start = ((), (), s32[]{:S(2)}) async-start(), calls=%async_computation.10 | async-start | bytes 3538944 | tf_op jit(solution)/shard_map/all_gather | solution.py:373
  14.3 272.9 %all-gather.15.cloned.1.call-start = ((), (), s32[]{:S(2)}) async-start(), calls=%async_computation.5 | async-start | bytes 4718592 | tf_op jit(solution)/shard_map/all_gather | solution.py:400
  198.2 89.0 %reduce-scatter.4.cloned.1.call-start = ((), (), s32[]{:S(2)}) async-start(), calls=%async_computation.6 | async-start | bytes 3538944 | tf_op jit(solution)/shard_map/reduce_scatter | solution.py:409
  246.8 79.4 %reduce-scatter.6.cloned.1.call-start = ((), (), s32[]{:S(2)}) async-start(), calls=%async_computation.7 | async-start | bytes 3538944 | tf_op jit(solution)/shard_map/reduce_scatter | solution.py:401
  247.4 158.6 %all-gather.13.cloned.1.call-start = ((), (), s32[]{:S(2)}) async-start(), calls=%async_computation.4 | async-start | bytes 9437184 | tf_op jit(solution)/shard_map/all_gather | solution.py:408
  248.1 237.6 %all-gather.11.cloned.1.call-start = ((), (), s32[]{:S(2)}) async-start(), calls=%async_computation.3 | async-start | bytes 9437184 | tf_op jit(solution)/shard_map/all_gather | solution.py:392
  248.9 293.6 %reduce-scatter.8.cloned.1.call-start = ((), (), s32[]{:S(2)}) async-start(), calls=%async_computation.8 | async-start | bytes 7077888 | tf_op jit(solution)/shard_map/reduce_scatter | solution.py:393
  545.2 7.0 %slice-start = ((s8[6291456]{0:T(1024)(128)(4,1)}), s8[2097152]{0:T(1024)(128)(4,1)S(1)}, s32[]{:S(2)}) async-start(s8[6291456]{0:T(1024)(128)(4,1)} %bitcast.38), calls=%async_computation.12 | async-start | bytes 4194304
  546.0 6.2 %slice-start.1 = ((s8[6291456]{0:T(1024)(128)(4,1)}), s8[4194304]{0:T(1024)(128)(4,1)S(1)}, s32[]{:S(2)}) async-start(s8[6291456]{0:T(1024)(128)(4,1)} %bitcast.38), calls=%async_computation.13 | async-start | bytes 8388608
  552.2 4.2 copy-start
Sparse Core Ops, SparseCore 0:
  10.4 23.1 all-gather.20
  36.0 19.9 all-gather.16
  58.4 26.9 all-gather.18
  198.3 42.1 all-gather.14
  246.9 38.4 reduce-scatter.3
  288.6 37.5 reduce-scatter.5
  327.7 78.2 all-gather.12
  407.5 78.2 all-gather.10
  489.6 52.7 reduce-scatter.7

commit v2 on v1

v2 whole, which is shorter than its diff:
```python
import functools
import math
import jax
import jax.numpy as jnp
from jax import lax
from jax.experimental import pallas as pl
from jax.experimental.pallas import tpu as pltpu
from jax.sharding import PartitionSpec as P

EPS = 1e-6
BUCKET_EDGES = tuple(math.ceil(16 * 8.0 ** (bucket_no / 16.0)) for bucket_no in range(1, 16))
NUM_BUCKETS = 32
D, INNER = 512, 384
T, E = 384, 192
PAIRS, BLK = 3, 128
ROW_OFF = (0, 128, 384)
F32, BF = jnp.float32, jnp.bfloat16
GELU_C = math.sqrt(2.0 / math.pi)
VMEM_LIMIT = 60 * 1024 * 1024


def nn(lhs, rhs):
    return lax.dot_general(lhs, rhs, (((1,), (0,)), ((), ())), preferred_element_type=F32)


def nt(lhs, rhs):
    return lax.dot_general(lhs, rhs, (((1,), (1,)), ((), ())), preferred_element_type=F32)


def tn(lhs, rhs):
    return lax.dot_general(lhs, rhs, (((0,), (0,)), ((), ())), preferred_element_type=F32)


def bf(val):
    return val.astype(BF)


def rounded(val):
    return val.astype(BF).astype(F32)


def unit_norm(act):
    act_f = act.astype(F32)
    inv_rms = lax.rsqrt(jnp.mean(act_f * act_f, axis=-1, keepdims=True) + EPS)
    return act_f * inv_rms, inv_rms


def norm_back(d_norm, unit_act, inv_rms, gain):
    d_norm_f = rounded(d_norm)
    d_unit = d_norm_f * gain
    d_act = inv_rms * (d_unit - unit_act * jnp.mean(d_unit * unit_act, axis=-1, keepdims=True))
    return d_act, jnp.sum(d_norm_f * unit_act, axis=0, keepdims=True)


def half_masks():
    lane = lax.broadcasted_iota(jnp.int32, (1, BLK), 1)
    low = jnp.where(lane < 64, 1.0, 0.0)
    return bf(low), bf(1.0 - low), lane < 64


def pick_half(low_rows, high_rows):
    lane = lax.broadcasted_iota(jnp.int32, low_rows.shape, 1)
    return jnp.where(lane < 64, low_rows, high_rows)


def pack_slots():
    for row in range(4):
        for half in range(2):
            for mat in range(4):
                first = mat * INNER + half * 192
                yield 4 * half + row, slice(mat * 192, (mat + 1) * 192), slice(first, first + 192), slice(row * BLK, (row + 1) * BLK)


def unpack(pack_ref, full_ref):
    for dev, rows, feats, cols in pack_slots():
        full_ref[feats, cols] = pack_ref[dev, rows, :]


def repack(full_ref, pack_ref):
    for dev, rows, feats, cols in pack_slots():
        pack_ref[dev, rows, :] = full_ref[feats, cols]


def bucket_block(diag):
    row = lax.broadcasted_iota(jnp.int32, (BLK, BLK), 0)
    col = lax.broadcasted_iota(jnp.int32, (BLK, BLK), 1)
    rel = row - col + diag * BLK
    bucket = jnp.clip(rel, 0, 16)
    for edge in BUCKET_EDGES:
        bucket = bucket + jnp.where(rel >= edge, 1, 0)
    return rel, bucket


def build_bias(table_ref, bias_ref):
    for diag in range(3):
        rel, bucket = bucket_block(diag)
        for head in range(6):
            row = jnp.broadcast_to(table_ref[head:head + 1, :], (BLK, BLK))
            vals = jnp.take_along_axis(row, bucket, axis=1, mode="promise_in_bounds")
            bias_ref[head, diag] = jnp.where(rel >= 0, vals, -jnp.inf)


def self_fwd(part_ref, pack_ref, gain_ref, table_ref, x_ref, x1_ref, qkv_ref, p_ref, ctx_ref, w_ref, bias_ref):
    @pl.when(pl.program_id(0) == 0)
    def _():
        unpack(pack_ref, w_ref)
        build_bias(table_ref, bias_ref)

    low, high, _ = half_masks()
    x_in = x_ref[0]
    unit_act, _ = unit_norm(x_in)
    normed = bf(unit_act * gain_ref[0:1, :])
    qkv_ref[0] = bf(nt(normed, w_ref[:3 * INNER]))
    for pair in range(PAIRS):
        lanes = pl.ds(pair * BLK, BLK)
        q_pair = qkv_ref[0, :, pl.ds(pair * BLK, BLK)]
        k_pair = qkv_ref[0, :, pl.ds(INNER + pair * BLK, BLK)]
        v_pair = qkv_ref[0, :, pl.ds(2 * INNER + pair * BLK, BLK)]
        k_heads = (k_pair * low, k_pair * high)
        v_heads = (v_pair * low, v_pair * high)
        for blk in range(3):
            keys = (blk + 1) * BLK
            q_rows = q_pair[blk * BLK:(blk + 1) * BLK]
            probs = []
            for sub in range(2):
                head = 2 * pair + sub
                bias = jnp.concatenate([bias_ref[head, blk - key_blk] for key_blk in range(blk + 1)], axis=1)
                logits = rounded(nt(q_rows, k_heads[sub][:keys])) + bias
                expd = jnp.exp(logits - jnp.max(logits, axis=1, keepdims=True))
                prob = expd * (1.0 / jnp.sum(expd, axis=1, keepdims=True))
                p_ref[0, head, :, ROW_OFF[blk]:ROW_OFF[blk] + keys] = prob
                probs.append(bf(prob))
            context = nn(jnp.concatenate(probs, axis=1), jnp.concatenate([v_heads[0][:keys], v_heads[1][:keys]], axis=0))
            ctx_ref[0, blk * BLK:(blk + 1) * BLK, lanes] = bf(context)
    x1_ref[0] = bf(x_in.astype(F32) + nn(ctx_ref[0], w_ref[3 * INNER:]))


def cross_mlp(begin, part_ref, pack_ref, mlp_ref, gain_ref, x1_ref, enc_ref, dy_ref, *refs):
    if not begin:
        mlp_in_ref, gain_in_ref, _, *refs = refs
    y_ref, yfull_ref, dmid_ref, q_ref, kv_ref, p_ref, ctx_ref, dmlp_ref, dgain_ref, w_ref, hid_ref, dpre_ref = refs

    @pl.when(pl.program_id(0) == 0)
    def _():
        unpack(pack_ref, w_ref)
        dmlp_ref[...] = jnp.zeros_like(dmlp_ref) if begin else mlp_in_ref[...]
        dgain_ref[...] = jnp.zeros_like(dgain_ref) if begin else gain_in_ref[...]

    low, high, _ = half_masks()
    unit_act, _ = unit_norm(x1_ref[0])
    normed = bf(unit_act * gain_ref[1:2, :])
    q_ref[0] = bf(nt(normed, w_ref[:INNER]))
    kv_ref[0] = bf(nt(enc_ref[0], w_ref[INNER:3 * INNER]))
    for pair in range(PAIRS):
        lanes = pl.ds(pair * BLK, BLK)
        q_pair = q_ref[0, :, lanes]
        k_pair = kv_ref[0, :, lanes]
        v_pair = kv_ref[0, :, pl.ds(INNER + pair * BLK, BLK)]
        k_heads = (k_pair * low, k_pair * high)
        probs = []
        for sub in range(2):
            logits = rounded(nt(k_heads[sub], q_pair))
            expd = jnp.exp(logits - jnp.max(logits, axis=0, keepdims=True))
            prob = expd * (1.0 / jnp.sum(expd, axis=0, keepdims=True))
            p_ref[0, 2 * pair + sub] = prob
            probs.append(bf(prob))
        context = tn(jnp.concatenate(probs, axis=0), jnp.concatenate([v_pair * low, v_pair * high], axis=0))
        ctx_ref[0, :, lanes] = bf(context)
    mid_2 = rounded(x1_ref[0].astype(F32) + nn(ctx_ref[0], w_ref[3 * INNER:]))

    unit_3, inv_3 = unit_norm(mid_2)
    gain_3 = gain_ref[2:3, :]
    normed_3 = bf(unit_3 * gain_3)
    dy = dy_ref[0]
    out = mid_2
    d_norm = jnp.zeros((T, D), F32)
    for half in range(2):
        wi_0, wi_1, wo_t = [jnp.concatenate([mlp_ref[4 * half + row, mat * BLK:(mat + 1) * BLK] for row in range(4)], axis=0) for mat in range(3)]
        pre_0 = rounded(nn(normed_3, wi_0))
        pre_1 = rounded(nn(normed_3, wi_1))
        d_hid = rounded(nn(dy, wo_t))
        sq = pre_0 * pre_0
        tanh = jnp.tanh(GELU_C * (pre_0 + 0.044715 * (sq * pre_0)))
        cdf = 0.5 * (1.0 + tanh)
        gelu = pre_0 * cdf
        slope = cdf + (0.5 * pre_0) * (1.0 - tanh * tanh) * (GELU_C * (1.0 + (3.0 * 0.044715) * sq))
        hid_ref[...] = bf(gelu * pre_1)
        dpre_ref[:, 0:512] = bf((d_hid * pre_1) * slope)
        dpre_ref[:, 512:1024] = bf(d_hid * gelu)
        out = out + nt(hid_ref[...], wo_t)
        d_norm = d_norm + nt(dpre_ref[:, 0:512], wi_0) + nt(dpre_ref[:, 512:1024], wi_1)
        grad_in = tn(normed_3, dpre_ref[...])
        grad_out = tn(dy, hid_ref[...])
        for row in range(4):
            rows = slice(row * BLK, (row + 1) * BLK)
            dmlp_ref[4 * half + row, 0:BLK] += grad_in[rows, 0:512]
            dmlp_ref[4 * half + row, BLK:2 * BLK] += grad_in[rows, 512:1024]
            dmlp_ref[4 * half + row, 2 * BLK:3 * BLK] += grad_out[rows]
    y_ref[0] = bf(out)
    yfull_ref[0] = y_ref[0]
    d_act, d_gain = norm_back(d_norm, unit_3, inv_3, gain_3)
    dgain_ref[...] += jnp.broadcast_to(d_gain, (8, D))
    dmid_ref[0] = bf(dy.astype(F32) + d_act)


def cross_bwd(begin, part_ref, pack_ref, gain_ref, x1_ref, enc_ref, dmid_ref, q_ref, kv_ref, p_ref, ctx_ref, *refs):
    if not begin:
        dw_in_ref, gain_in_ref, _, *refs = refs
    dx1_ref, denc_ref, dencfull_ref, dw_ref, dgain_ref, w_ref, acc_ref, dq_ref, dkv_ref, dctx_ref = refs
    step = pl.program_id(0)

    @pl.when(step == 0)
    def _():
        unpack(pack_ref, w_ref)
        if begin:
            acc_ref[...] = jnp.zeros_like(acc_ref)
        else:
            unpack(dw_in_ref, acc_ref)
        dgain_ref[...] = jnp.zeros_like(dgain_ref) if begin else gain_in_ref[...]

    low, high, _ = half_masks()
    d_mid = dmid_ref[0]
    dctx_ref[...] = bf(nt(d_mid, w_ref[3 * INNER:]))
    acc_ref[3 * INNER:] += tn(ctx_ref[0], d_mid)
    for pair in range(PAIRS):
        lanes = pl.ds(pair * BLK, BLK)
        q_pair = q_ref[0, :, lanes]
        k_pair = kv_ref[0, :, lanes]
        v_pair = kv_ref[0, :, pl.ds(INNER + pair * BLK, BLK)]
        dctx_pair = dctx_ref[:, lanes]
        v_heads = (v_pair * low, v_pair * high)
        probs, d_logits = [], []
        for sub in range(2):
            prob = p_ref[0, 2 * pair + sub]
            d_prob = rounded(nt(v_heads[sub], dctx_pair))
            delta = jnp.sum(prob * d_prob, axis=0, keepdims=True)
            d_logits.append(bf(prob * (d_prob - delta)))
            probs.append(bf(prob))
        d_logit = jnp.concatenate(d_logits, axis=0)
        dq_ref[:, lanes] = bf(tn(d_logit, jnp.concatenate([k_pair * low, k_pair * high], axis=0)))
        dk_both = nn(d_logit, q_pair)
        dkv_ref[:, lanes] = bf(pick_half(dk_both[:E], dk_both[E:]))
        dv_both = nn(jnp.concatenate(probs, axis=0), dctx_pair)
        dkv_ref[:, pl.ds(INNER + pair * BLK, BLK)] = bf(pick_half(dv_both[:E], dv_both[E:]))
    denc_ref[0] = bf(nn(dkv_ref[...], w_ref[INNER:3 * INNER]))
    dencfull_ref[0] = denc_ref[0]
    acc_ref[INNER:3 * INNER] += tn(dkv_ref[...], enc_ref[0])
    unit_act, inv_rms = unit_norm(x1_ref[0])
    gain = gain_ref[1:2, :]
    acc_ref[:INNER] += tn(dq_ref[...], bf(unit_act * gain))
    d_act, d_gain = norm_back(nn(dq_ref[...], w_ref[:INNER]), unit_act, inv_rms, gain)
    dgain_ref[...] += jnp.broadcast_to(d_gain, (8, D))
    dx1_ref[0] = bf(d_mid.astype(F32) + d_act)

    @pl.when(step == pl.num_programs(0) - 1)
    def _():
        repack(acc_ref, dw_ref)


def self_bwd(begin, part_ref, pack_ref, gain_ref, x_ref, dmid_ref, qkv_ref, p_ref, ctx_ref, *refs):
    if not begin:
        dw_in_ref, gain_in_ref, bias_in_ref, _, *refs = refs
    dx_ref, dxfull_ref, dw_ref, dgain_ref, dbias_ref, w_ref, acc_ref, dqkv_ref, dctx_ref = refs
    step = pl.program_id(0)

    @pl.when(step == 0)
    def _():
        unpack(pack_ref, w_ref)
        if begin:
            acc_ref[...] = jnp.zeros_like(acc_ref)
        else:
            unpack(dw_in_ref, acc_ref)
        dgain_ref[...] = jnp.zeros_like(dgain_ref) if begin else gain_in_ref[...]
        dbias_ref[...] = jnp.zeros_like(dbias_ref) if begin else bias_in_ref[...]

    low, high, _ = half_masks()
    d_mid = dmid_ref[0]
    dctx_ref[...] = bf(nt(d_mid, w_ref[3 * INNER:]))
    acc_ref[3 * INNER:] += tn(ctx_ref[0], d_mid)
    for pair in range(PAIRS):
        q_pair = qkv_ref[0, :, pl.ds(pair * BLK, BLK)]
        k_pair = qkv_ref[0, :, pl.ds(INNER + pair * BLK, BLK)]
        v_pair = qkv_ref[0, :, pl.ds(2 * INNER + pair * BLK, BLK)]
        dctx_pair = dctx_ref[:, pl.ds(pair * BLK, BLK)]
        k_heads = (k_pair * low, k_pair * high)
        v_heads = (v_pair * low, v_pair * high)
        probs, d_logits = [[], []], [[], []]
        for blk in range(3):
            keys = (blk + 1) * BLK
            for sub in range(2):
                head = 2 * pair + sub
                prob = p_ref[0, head, :, ROW_OFF[blk]:ROW_OFF[blk] + keys]
                d_prob = rounded(nt(dctx_pair[blk * BLK:(blk + 1) * BLK], v_heads[sub][:keys]))
                delta = jnp.sum(prob * d_prob, axis=1, keepdims=True)
                d_logit = prob * (d_prob - delta)
                for key_blk in range(blk + 1):
                    dbias_ref[head, blk - key_blk] += d_logit[:, key_blk * BLK:(key_blk + 1) * BLK]
                d_logits[sub].append(bf(d_logit))
                probs[sub].append(bf(prob))
            d_query = nn(jnp.concatenate([d_logits[0][blk], d_logits[1][blk]], axis=1),
                         jnp.concatenate([k_heads[0][:keys], k_heads[1][:keys]], axis=0))
            dqkv_ref[blk * BLK:(blk + 1) * BLK, pl.ds(pair * BLK, BLK)] = bf(d_query)
        for vals, rhs, base in ((d_logits, q_pair, INNER), (probs, dctx_pair, 2 * INNER)):
            for key_blk in range(3):
                cols = slice(key_blk * BLK, (key_blk + 1) * BLK)
                left = jnp.concatenate([jnp.concatenate([vals[sub][blk][:, cols] for blk in range(key_blk, 3)], axis=0) for sub in range(2)], axis=1)
                both = tn(left, rhs[key_blk * BLK:])
                dqkv_ref[cols, pl.ds(base + pair * BLK, BLK)] = bf(pick_half(both[:BLK], both[BLK:]))
    unit_act, inv_rms = unit_norm(x_ref[0])
    gain = gain_ref[0:1, :]
    acc_ref[:3 * INNER] += tn(dqkv_ref[...], bf(unit_act * gain))
    d_act, d_gain = norm_back(nn(dqkv_ref[...], w_ref[:3 * INNER]), unit_act, inv_rms, gain)
    dgain_ref[...] += jnp.broadcast_to(d_gain, (8, D))
    dx_ref[0] = bf(d_mid.astype(F32) + d_act)
    dxfull_ref[0] = dx_ref[0]

    @pl.when(step == pl.num_programs(0) - 1)
    def _():
        repack(acc_ref, dw_ref)


def bucket_sums(dbias_ref, dg1_ref, dg2_ref, dg3_ref, out_ref):
    blocks = [bucket_block(diag) for diag in range(3)]
    buckets = [jnp.where(rel >= 0, bucket, -1) for rel, bucket in blocks]

    lane = lax.broadcasted_iota(jnp.int32, (8, BLK), 1)

    def one_bucket(bucket_no, sums):
        rows = []
        for head in range(6):
            total = jnp.zeros((BLK, BLK), F32)
            for diag in range(3):
                total = total + jnp.where(buckets[diag] == bucket_no, dbias_ref[head, diag], 0.0)
            rows.append(jnp.sum(total, axis=0, keepdims=True))
        rows += [jnp.zeros((1, BLK), F32)] * 2
        per_head = jnp.sum(jnp.concatenate(rows, axis=0), axis=1, keepdims=True)
        return jnp.where(lane == bucket_no, per_head, sums)

    out_ref[:, D:] = lax.fori_loop(0, NUM_BUCKETS, one_bucket, jnp.zeros((8, BLK), F32))
    row = lax.broadcasted_iota(jnp.int32, (8, D), 0)
    out_ref[:, :D] = jnp.where(row == 0, dg1_ref[...], jnp.where(row == 1, dg2_ref[...], dg3_ref[...]))


def seq_block(first, *dims):
    zeros = (0,) * len(dims)
    return pl.BlockSpec((1,) + dims, lambda i, part: (first + i,) + zeros)


def arg_block(first, *dims):
    zeros = (0,) * len(dims)
    return pl.BlockSpec((1,) + dims, lambda i, part: (part[0] * 8 + first + i,) + zeros)


def whole(*dims):
    zeros = (0,) * len(dims)
    return pl.BlockSpec(dims, lambda i, part: zeros)


def shape(dims, dtype):
    return jax.ShapeDtypeStruct(dims, dtype)


def whole_out(dims, dtype):
    return whole(*dims), shape(dims, dtype)


def call(body, seqs, flops, in_specs, outs, scratch, args, aliases=None):
    out_specs, out_shape = zip(*outs)
    return pl.pallas_call(
        body,
        out_shape=out_shape,
        grid_spec=pltpu.PrefetchScalarGridSpec(num_scalar_prefetch=1, grid=(seqs,), in_specs=in_specs, out_specs=out_specs, scratch_shapes=scratch),
        input_output_aliases=aliases or {},
        compiler_params=pltpu.CompilerParams(dimension_semantics=("arbitrary",), vmem_limit_bytes=VMEM_LIMIT),
        cost_estimate=pl.CostEstimate(flops=flops * seqs, bytes_accessed=5_000_000 * seqs, transcendentals=0),
    )(*args)


def layer_shard(dec_in, enc_out, grad_out, rel_bias, self_q, self_k, self_v, self_o, cross_q, cross_k, cross_v, cross_o, mlp_wi_0, mlp_wi_1, mlp_wo, norm_self, norm_cross, norm_mlp):
    axes = ("model", "data")
    batch = dec_in.shape[0]
    seqs = batch // 2
    chunk = seqs // 2
    part = lax.axis_index("model").astype(jnp.int32).reshape(1)
    rows = (norm_self[None], norm_cross[None], norm_mlp[None], jnp.pad(rel_bias.T, ((0, 0), (0, BLK - NUM_BUCKETS))))
    small = sum(jnp.pad(val, ((pos, 16 - pos - val.shape[0]), (0, 0))) for pos, val in enumerate(rows))
    small = lax.all_gather(small, axes).astype(F32)
    gains = small[:4].transpose(1, 0, 2).reshape(16, D)[:8]
    table = small[:, 3:6].reshape(2, 4, 3, BLK)[:, 0].reshape(6, BLK)
    table = jnp.pad(table, ((0, 2), (0, 0)))
    w_self = lax.all_gather(jnp.concatenate([self_q.T, self_k.T, self_v.T, self_o], axis=0), axes)
    w_cross = lax.all_gather(jnp.concatenate([cross_q.T, cross_k.T, cross_v.T, cross_o], axis=0), axes)
    w_mlp = lax.all_gather(jnp.concatenate([mlp_wi_0, mlp_wi_1, mlp_wo.T], axis=0), axes)

    vmem = pltpu.VMEM
    pack_spec = whole(8, 768, BLK)
    any_spec = pl.BlockSpec(memory_space=pl.ANY)
    w_scr = vmem((1536, D), BF)
    acc_scr = vmem((1536, D), F32)
    full_out = {rows: shape((batch, rows, D), BF) for rows in (T, E)}
    model_no = lax.axis_index("model")

    def seq_out(count, dims, dtype):
        return seq_block(0, *dims), shape((count,) + dims, dtype)

    def send(val):
        return lax.ppermute(val, "model", [(0, 1), (1, 0)])

    def scatter(val):
        return lax.psum_scatter(val, axes, scatter_dimension=0)

    def place(full, received):
        for pos, val in enumerate(received):
            full = lax.dynamic_update_slice(full, val, ((1 - model_no) * seqs + pos * chunk, 0, 0))
        return full

    mid_1, qkv, probs, ctx = call(
        self_fwd, seqs, 7_000_000_000,
        [pack_spec, whole(8, D), whole(8, BLK), arg_block(0, T, D)],
        [seq_out(seqs, (T, D), BF), seq_out(seqs, (T, 3 * INNER), BF), seq_out(seqs, (6, BLK, 768), F32), seq_out(seqs, (T, INNER), BF)],
        [w_scr, vmem((6, 3, BLK, BLK), F32)],
        (part, w_self, gains, table, dec_in))

    saved, got_y, chain = [], [], ()
    for pos in range(2):
        first = pos * chunk
        extra = [whole(8, 384, D), whole(8, D), any_spec] if pos else []
        y_part, y_full, d_mid, q_x, kv_x, probs_x, ctx_x, d_mlp, d_gain_3 = call(
            functools.partial(cross_mlp, pos == 0), chunk, 14_000_000_000,
            [pack_spec, whole(8, 384, D), whole(8, D), seq_block(first, T, D), arg_block(first, E, D), arg_block(first, T, D)] + extra,
            [seq_out(chunk, (T, D), BF), (arg_block(first, T, D), full_out[T]), seq_out(chunk, (T, D), BF), seq_out(chunk, (T, INNER), BF), seq_out(chunk, (E, 2 * INNER), BF),
             seq_out(chunk, (6, E, T), F32), seq_out(chunk, (T, INNER), BF), whole_out((8, 384, D), F32), whole_out((8, D), F32)],
            [w_scr, vmem((T, 512), BF), vmem((T, 1024), BF)],
            (part, w_cross, w_mlp, gains, mid_1, enc_out, grad_out) + chain, {9: 1} if pos else None)
        chain = (d_mlp, d_gain_3, y_full)
        got_y.append(send(y_part))
        saved.append((d_mid, q_x, kv_x, probs_x, ctx_x))
    d_mlp = scatter(d_mlp)

    d_mids, got_e, chain = [], [], ()
    for pos in range(2):
        first = pos * chunk
        extra = [pack_spec, whole(8, D), any_spec] if pos else []
        d_mid_1, e_part, e_full, d_cross, d_gain_2 = call(
            functools.partial(cross_bwd, pos == 0), chunk, 7_000_000_000,
            [pack_spec, whole(8, D), seq_block(first, T, D), arg_block(first, E, D), seq_block(0, T, D), seq_block(0, T, INNER), seq_block(0, E, 2 * INNER), seq_block(0, 6, E, T), seq_block(0, T, INNER)] + extra,
            [seq_out(chunk, (T, D), BF), seq_out(chunk, (E, D), BF), (arg_block(first, E, D), full_out[E]), whole_out((8, 768, BLK), F32), whole_out((8, D), F32)],
            [w_scr, acc_scr, vmem((T, INNER), BF), vmem((E, 2 * INNER), BF), vmem((T, INNER), BF)],
            (part, w_cross, gains, mid_1, enc_out) + saved[pos] + chain, {12: 2} if pos else None)
        chain = (d_cross, d_gain_2, e_full)
        got_e.append(send(e_part))
        d_mids.append(d_mid_1)
    d_cross = scatter(d_cross)

    got_x, chain = [], ()
    for pos in range(2):
        first = pos * chunk
        extra = [pack_spec, whole(8, D), whole(6, 3, BLK, BLK), any_spec] if pos else []
        x_part, x_full, d_self, d_gain_1, d_bias = call(
            functools.partial(self_bwd, pos == 0), chunk, 11_000_000_000,
            [pack_spec, whole(8, D), arg_block(first, T, D), seq_block(0, T, D), seq_block(first, T, 3 * INNER), seq_block(first, 6, BLK, 768), seq_block(first, T, INNER)] + extra,
            [seq_out(chunk, (T, D), BF), (arg_block(first, T, D), full_out[T]), whole_out((8, 768, BLK), F32), whole_out((8, D), F32), whole_out((6, 3, BLK, BLK), F32)],
            [w_scr, acc_scr, vmem((T, 3 * INNER), BF), vmem((T, INNER), BF)],
            (part, w_self, gains, dec_in, d_mids[pos], qkv, probs, ctx) + chain, {11: 1} if pos else None)
        chain = (d_self, d_gain_1, d_bias, x_full)
        got_x.append(send(x_part))
    d_self = scatter(d_self)

    tiny = pl.pallas_call(bucket_sums, name="bucket_sums", out_shape=shape((8, D + BLK), F32))(d_bias, d_gain_1, d_gain_2, d_gain_3)
    tiny = lax.psum(tiny, axes)
    data_no = lax.axis_index("data")
    gain_grads = lax.dynamic_slice(tiny, (0, data_no * BLK), (3, BLK))
    gain_grads = (gain_grads[0], gain_grads[1], gain_grads[2])
    bias_sums = tiny[:, D:D + NUM_BUCKETS]
    grad_bias = jnp.where(model_no == 0, bias_sums[0:3], bias_sums[3:6]).T

    dec_out, grad_enc, grad_dec = place(y_full, got_y), place(e_full, got_e), place(x_full, got_x)

    def split_attn(grad_pack):
        mats = [grad_pack[192 * pos:192 * (pos + 1)] for pos in range(4)]
        return mats[0].T, mats[1].T, mats[2].T, mats[3]

    return (dec_out, grad_dec, grad_enc, grad_bias) + split_attn(d_self) + split_attn(d_cross) + (
        d_mlp[:BLK], d_mlp[BLK:2 * BLK], d_mlp[2 * BLK:].T) + gain_grads


def solution(mesh):
    row_spec = P("data", None, None)
    col_in = P("data", "model")
    col_out = P("model", "data")
    gain_spec = P("data")
    bias_spec = P(None, "model")
    arg_specs = (row_spec, row_spec, row_spec, bias_spec, col_in, col_in, col_in, col_out, col_in, col_in, col_in, col_out, col_in, col_in, col_out, gain_spec, gain_spec, gain_spec)
    out_specs = (row_spec, row_spec, row_spec) + arg_specs[3:]

    return jax.shard_map(layer_shard, mesh=mesh, in_specs=arg_specs, out_specs=out_specs, check_vma=False)
```

time: 565 us -> 528 us (0.935); the launches traced: 565 us -> 519 us
  waiting for transfers between devices: 272 us -> 33.1 us
  blocking collectives: 37 us -> 206 us
  Pallas kernels: 191 us -> 225 us
  local copies, waits for them, and re-layouts: 44.2 us -> 26.7 us
  starting transfers between devices: 0.36 us -> 8.23 us
    psum x1, blocking collectives: 23 us -> 194 us  [layer_shard(): tiny = lax.psum(tiny, axes)]
    all_gather x6 -> x3, waiting for transfers between devices: 178 us -> 14.1 us  [the longest x1 9.44 us: layer_shard(): lax.all_gather(jnp.concatenate([cross_q.T, cross_k.T, cross_v.T, cross_o]...]
    reduce_scatter x3, waiting for transfers between devices: 91.5 us -> 0.01 us  [scatter(): return lax.psum_scatter(val, axes, scatter_dimension=0)]
    pallas_call x4 -> x7, Pallas kernels: 183 us -> 217 us  [call(): pl.pallas_call(body, out_shape=out_shape, grid_spec=pltpu.PrefetchScalarG...]
    unnamed x22 -> x4, local copies, waits for them, and re-layouts: 21.7 us -> 2.89 us
    ppermute x0 -> x6, waiting for transfers between devices: none -> 18.4 us  [send(): return lax.ppermute(val, 'model', [(0, 1), (1, 0)])]
    dynamic_update_slice x0 -> x6, local copies, waits for them, and re-layouts: none -> 11.9 us  [place(): lax.dynamic_update_slice(full, val, ((1 - model_no) * seqs + pos * chunk,...]
    ppermute x0 -> x6, starting transfers between devices: none -> 7.98 us  [send(): return lax.ppermute(val, 'model', [(0, 1), (1, 0)])]
  transfers between devices with their start and end apart: 9 -> 12, of which waited for: 6 -> 3; matrix products, arithmetic and copies ran while one was open for 5% -> 5% of each run, Pallas kernels for 17% -> 20%
where the time goes in v2:
time: 528 us; the launch traced here: 519 us
  Pallas kernels  225 us (43%)
  blocking collectives  206 us (39%)
  waiting for transfers between devices  33.1 us (6%)
  local copies, waits for them, and re-layouts  26.7 us (5%)
  between operations  14.6 us (3%)
  starting transfers between devices  8.23 us (2%)
  other arithmetic  6.14 us (1%)
    pallas_call x7, Pallas kernels, call(): pl.pallas_call(body, out_shape=out_shape, grid_spec=pltpu.PrefetchScalarG...  217 us
    psum x1, blocking collectives, layer_shard(): tiny = lax.psum(tiny, axes)  194 us
    ppermute x6, waiting for transfers between devices, send(): return lax.ppermute(val, 'model', [(0, 1), (1, 0)])  18.4 us
    all_gather x1, blocking collectives, layer_shard(): small = lax.all_gather(small, axes).astype(F32)  12.3 us
    dynamic_update_slice x6, local copies, waits for them, and re-layouts, place(): lax.dynamic_update_slice(full, val, ((1 - model_no) * seqs + pos * chunk,...  11.9 us
  transfers between devices with their start and end apart: 12, of which 3 were waited for; matrix products, arithmetic and copies ran while one was open for 5% of the time, Pallas kernels for 20%

profile of v2, /device:TPU:0, one launch (start us, length us, event | category | flops | bytes accessed | tf_op | source)
XLA Modules:
  0.0 519.2 jit_solution(13646033230200602935)
XLA Ops:
  7.2 0.0 all-gather.12.cloned.1.call-start
  7.2 1.6 pad_maximum_fusion.2
  8.8 0.0 all-gather.12.cloned.1.call-update
  8.8 0.0 all-gather.10.cloned.1.call-start
  8.9 1.0 copy.43
  9.9 1.0 copy.44
  10.9 1.7 pad_maximum_fusion
  12.6 0.0 all-gather.10.cloned.1.call-update
  12.7 0.0 all-gather.8.cloned.1.call-start
  12.7 1.6 pad_maximum_fusion.1
  14.3 0.0 all-gather.8.cloned.1.call-update
  14.3 0.0 reduce-scatter.6.cloned.1.call-start
  14.4 0.7 pad_add_fusion
  15.1 12.3 %all-gather.2 = bf16[128,128]{1,0:T(8,128)(2,1)S(1)} all-gather(bf16[16,128]{1,0:T(8,128)(2,1)S(1)} %pad_add_fusion), channel_id=4, replica_groups=mesh['model'=2,'data'=4] {'model','data'}, dimensions={0}, use_global_device_ids=true | all-gather | bytes 36864 | tf_op jit(solution)/shard_map/all_gather | solution.py:387
  27.4 0.6 slice_bitcast_fusion.11.gain_ref
  28.0 0.6 pad.29.table_ref
  28.6 4.7 all-gather.12.cloned.1.call-done
  33.3 38.0 %shard_map.313 = (bf16[8,384,512]{2,1,0:T(8,128)(2,1)}, bf16[8,384,1152]{2,1,0:T(8,128)(2,1)}, f32[8,6,128,768]{3,2,1,0:T(8,128)}, bf16[8,384,384]{2,1,0:T(8,128)(2,1)}) custom-call(s32[1]{0:T(128)} %bitcast.part_ref, bf16[8,768,128]{2,1,0:T(8,128)(2,1)} %bitcast.84, f32[8,512]{1,0:T(8,128)} %slice_bitcast_fusion.11.gain_ref, f32[8,128]{1,0:T(8,128)} %pad.29.table_ref, ...), custom_call_target="tpu_custom_call" | custom-call | flops 56000000000 | bytes 40000000 | tf_op jit(solution)/shard_map/pallas_call | solution.py:369
  71.3 0.0 all-gather.10.cloned.1.call-done
  71.3 4.6 copy.45
  76.0 9.4 %all-gather.8.cloned.1.call-done = bf16[6144,128]{1,0:T(8,128)(2,1)} async-done(((bf16[768,128]{1,0:T(8,128)(2,1)}), bf16[6144,128]{1,0:T(8,128)(2,1)}) %all-gather.8.cloned.1.call-update) | async-done | bytes 1572880 | tf_op jit(solution)/shard_map/all_gather | solution.py:392
  85.4 35.1 %shard_map.314 = (bf16[4,384,512]{2,1,0:T(8,128)(2,1)}, bf16[16,384,512]{2,1,0:T(8,128)(2,1)}, bf16[4,384,512]{2,1,0:T(8,128)(2,1)}, bf16[4,384,384]{2,1,0:T(8,1...) custom-call(s32[1]{0:T(128)} %bitcast.part_ref, ...), custom_call_target="tpu_custom_call" | custom-call | flops 56000000000 | bytes 20000000 | tf_op jit(solution)/shard_map/pallas_call | solution.py:369
  120.5 47.3 %shard_map.315 = (bf16[4,384,512]{2,1,0:T(8,128)(2,1)}, bf16[16,384,512]{2,1,0:T(8,128)(2,1)}, bf16[4,384,512]{2,1,0:T(8,128)(2,1)}, bf16[4,384,384]{2,1,0:T(8,1...) custom-call(s32[1]{0:T(128)} %bitcast.part_ref, ...), custom_call_target="tpu_custom_call", output_to_operand_aliasing={{1}: (9, {})} | custom-call | flops 56000000000 | bytes 20000000 | tf_op jit(solution)/shard_map/pallas_call | solution.py:369
  167.8 18.9 %shard_map.316 = (bf16[4,384,512]{2,1,0:T(8,128)(2,1)}, bf16[4,192,512]{2,1,0:T(8,128)(2,1)}, bf16[16,192,512]{2,1,0:T(8,128)(2,1)}, f32[8,768,128]{2,1,0:T(8,128)}, f32[8,512]{1,0:T(8,128)}) custom-call(s32[1]{0:T(128)} %bitcast.part_ref, bf16[8,768,128]{2,1,0:T(8,128)(2,1)} %bitcast.89, f32[8,512]{1,0:T(8,128)} %slice_bitcast_fusion.11.gain_ref, ...), custom_call_target="tpu_custom_call" | custom-call | flops 28000000000 | bytes 20000000 | tf_op jit(solution)/shard_map/pallas_call | solution.py:369
  186.7 20.2 %shard_map.317 = (bf16[4,384,512]{2,1,0:T(8,128)(2,1)}, bf16[4,192,512]{2,1,0:T(8,128)(2,1)}, bf16[16,192,512]{2,1,0:T(8,128)(2,1)}, f32[8,768,128]{2,1,0:T(8,128)}, f32[8,512]{1,0:T(8,128)}) custom-call(s32[1]{0:T(128)} %bitcast.part_ref, bf16[8,768,128]{2,1,0:T(8,128)(2,1)} %bitcast.90, ...), custom_call_target="tpu_custom_call", output_to_operand_aliasing={{2}: (12, {})} | custom-call | flops 28000000000 | bytes 20000000 | tf_op jit(solution)/shard_map/pallas_call | solution.py:369
  206.9 0.0 reduce-scatter.6.cloned.1.call-update
  206.9 0.0 reduce-scatter.4.cloned.1.call-start
  206.9 28.1 %shard_map.318 = (bf16[4,384,512]{2,1,0:T(8,128)(2,1)}, bf16[16,384,512]{2,1,0:T(8,128)(2,1)}, f32[8,768,128]{2,1,0:T(8,128)}, f32[8,512]{1,0:T(8,128)}, f32[6,3,128,128]{3,2,1,0:T(8,128)}) custom-call(s32[1]{0:T(128)} %bitcast.part_ref, bf16[8,768,128]{2,1,0:T(8,128)(2,1)} %bitcast.85, f32[8,512]{1,0:T(8,128)} %slice_bitcast_fusion.11.gain_ref, ...), custom_call_target="tpu_custom_call" | custom-call | flops 44000002048 | bytes 20000000 | tf_op jit(solution)/shard_map/pallas_call | solution.py:369
  235.1 29.5 %shard_map.319 = (bf16[4,384,512]{2,1,0:T(8,128)(2,1)}, bf16[16,384,512]{2,1,0:T(8,128)(2,1)}, f32[8,768,128]{2,1,0:T(8,128)}, f32[8,512]{1,0:T(8,128)}, f32[6,3,128,128]{3,2,1,0:T(8,128)}) custom-call(s32[1]{0:T(128)} %bitcast.part_ref, bf16[8,768,128]{2,1,0:T(8,128)(2,1)} %bitcast.86, ...), custom_call_target="tpu_custom_call", output_to_operand_aliasing={{1}: (11, {})} | custom-call | flops 44000002048 | bytes 20000000 | tf_op jit(solution)/shard_map/pallas_call | solution.py:369
  264.5 0.0 reduce-scatter.4.cloned.1.call-update
  264.6 0.0 reduce-scatter.8.cloned.1.call-start
  264.6 0.5 reduce-scatter.8.cloned.1.call-update
  265.1 1.4 collective-permute-start.4
  266.6 0.6 collective-permute-start
  267.2 1.4 collective-permute-start.1
  268.6 0.6 collective-permute-start.2
  269.2 1.4 collective-permute-start.3
  270.6 18.3 %collective-permute-done.4 = bf16[4,192,512]{2,1,0:T(8,128)(2,1)} collective-permute-done((bf16[4,192,512]{2,1,0:T(8,128)(2,1)}, bf16[4,192,512]{2,1,0:T(8,128)(2,1)}, u32[]{:S(2)}, u32[]{:S(2)}) %collective-permute-start.4) | collective-permute-done | bytes 786464 | tf_op jit(solution)/shard_map/ppermute | solution.py:407
  289.0 2.5 collective-permute-start.5
  291.5 7.6 %bucket_sums.1 = f32[8,640]{1,0:T(8,128)} custom-call(f32[6,3,128,128]{3,2,1,0:T(8,128)} %get-tuple-element.95.dbias_ref, f32[8,512]{1,0:T(8,128)} %get-tuple-element.96.dg1_ref, f32[8,512]{1,0:T(8,128)} %get-tuple-element.97.dg2_ref, f32[8,512]{1,0:T(8,128)} %get-tuple-element.98.dg3_ref), custom_call_target="tpu_custom_call" | custom-call | tf_op jit(solution)/shard_map/bucket_sums/pallas_call | solution.py:469
  299.0 193.6 %psum.7 = f32[8,640]{1,0:T(8,128)S(1)} all-reduce(f32[8,640]{1,0:T(8,128)} %bucket_sums.1), channel_id=1, replica_groups=mesh['model'=2,'data'=4] {'model','data'}, use_global_device_ids=true, to_apply=%region_0.1 | all-reduce | flops 5120 | bytes 40960 | tf_op jit(solution)/shard_map/psum | solution.py:470
  492.6 0.5 slice_bitcast_fusion.12
  493.2 0.6 fusion
  493.7 2.1 constant_dynamic-update-slice_fusion.1
  495.8 0.0 collective-permute-done.5
  495.8 2.1 constant_dynamic-update-slice_fusion
  497.9 0.0 collective-permute-done
  497.9 2.7 constant_dynamic-update-slice_fusion.5
  500.5 0.0 collective-permute-done.1
  500.5 2.7 constant_dynamic-update-slice_fusion.4
  503.2 0.0 collective-permute-done.2
  503.2 1.2 constant_dynamic-update-slice_fusion.3
  504.4 0.0 collective-permute-done.3
  504.4 1.2 constant_dynamic-update-slice_fusion.2
  505.7 0.0 reduce-scatter.6.cloned.1.call-done
  505.7 1.8 slice_bitcast_fusion.3
  507.5 0.0 reduce-scatter.4.cloned.1.call-done
  507.5 1.8 slice_bitcast_fusion.7
  509.2 0.0 reduce-scatter.8.cloned.1.call-done
  509.2 1.9 slice_bitcast_fusion
  511.2 0.8 copy.48
  (8 shorter events, 0.0 us)
Async XLA Ops:
  7.2 26.1 %all-gather.12.cloned.1.call-start = ((), (), s32[]{:S(2)}) async-start(), calls=%async_computation.8 | async-start | bytes 1769472 | tf_op jit(solution)/shard_map/all_gather | solution.py:391
  8.8 62.5 %all-gather.10.cloned.1.call-start = ((), (), s32[]{:S(2)}) async-start(), calls=%async_computation.7 | async-start | bytes 3538944 | tf_op jit(solution)/shard_map/all_gather | solution.py:393
  12.7 72.7 %all-gather.8.cloned.1.call-start = ((), (), s32[]{:S(2)}) async-start(), calls=%async_computation.6 | async-start | bytes 1769472 | tf_op jit(solution)/shard_map/all_gather | solution.py:392
  14.3 491.4 %reduce-scatter.6.cloned.1.call-start = ((), (), s32[]{:S(2)}) async-start(), calls=%async_computation.4 | async-start | bytes 3538944 | tf_op jit(solution)/shard_map/reduce_scatter | solution.py:410
  206.9 300.6 %reduce-scatter.4.cloned.1.call-start = ((), (), s32[]{:S(2)}) async-start(), calls=%async_computation.3 | async-start | bytes 3538944 | tf_op jit(solution)/shard_map/reduce_scatter | solution.py:410
  264.6 244.7 %reduce-scatter.8.cloned.1.call-start = ((), (), s32[]{:S(2)}) async-start(), calls=%async_computation.5 | async-start | bytes 7077888 | tf_op jit(solution)/shard_map/reduce_scatter | solution.py:410
  265.1 23.8 %collective-permute-start.4 = (bf16[4,192,512]{2,1,0:T(8,128)(2,1)}, bf16[4,192,512]{2,1,0:T(8,128)(2,1)}, u32[]{:S(2)}, u32[]{:S(2)}) collective-permute-start(bf16[4,192,512]{2,1,0:T(8,128)(2,1)} %get-tuple-element.93), channel_id=1, source_target_pairs={{0,4},{4,0},{1,5},{5,1},{2,6},{6,2},{3,7},{7,3}} | collective-permute-start | bytes 2359304 | tf_op jit(solution)/shard_map/ppermute | solution.py:407
  266.6 231.3 %collective-permute-start = (bf16[4,384,512]{2,1,0:T(8,128)(2,1)}, bf16[4,384,512]{2,1,0:T(8,128)(2,1)}, u32[]{:S(2)}, u32[]{:S(2)}) collective-permute-start(bf16[4,384,512]{2,1,0:T(8,128)(2,1)} %get-tuple-element.65), channel_id=1, source_target_pairs={{0,4},{4,0},{1,5},{5,1},{2,6},{6,2},{3,7},{7,3}} | collective-permute-start | bytes 4718600 | tf_op jit(solution)/shard_map/ppermute | solution.py:407
  267.2 233.3 %collective-permute-start.1 = (bf16[4,384,512]{2,1,0:T(8,128)(2,1)}, bf16[4,384,512]{2,1,0:T(8,128)(2,1)}, u32[]{:S(2)}, u32[]{:S(2)}) collective-permute-start(bf16[4,384,512]{2,1,0:T(8,128)(2,1)} %get-tuple-element.66), channel_id=1, source_target_pairs={{0,4},{4,0},{1,5},{5,1},{2,6},{6,2},{3,7},{7,3}} | collective-permute-start | bytes 4718600 | tf_op jit(solution)/shard_map/ppermute | solution.py:407
  268.6 234.6 %collective-permute-start.2 = (bf16[4,384,512]{2,1,0:T(8,128)(2,1)}, bf16[4,384,512]{2,1,0:T(8,128)(2,1)S(1)}, u32[]{:S(2)}, u32[]{:S(2)}) collective-permute-start(bf16[4,384,512]{2,1,0:T(8,128)(2,1)} %get-tuple-element.90), channel_id=1, source_target_pairs={{0,4},{4,0},{1,5},{5,1},{2,6},{6,2},{3,7},{7,3}} | collective-permute-start | bytes 4718600 | tf_op jit(solution)/shard_map/ppermute | solution.py:407
  269.2 235.2 %collective-permute-start.3 = (bf16[4,384,512]{2,1,0:T(8,128)(2,1)}, bf16[4,384,512]{2,1,0:T(8,128)(2,1)S(1)}, u32[]{:S(2)}, u32[]{:S(2)}) collective-permute-start(bf16[4,384,512]{2,1,0:T(8,128)(2,1)} %get-tuple-element.91), channel_id=1, source_target_pairs={{0,4},{4,0},{1,5},{5,1},{2,6},{6,2},{3,7},{7,3}} | collective-permute-start | bytes 4718600 | tf_op jit(solution)/shard_map/ppermute | solution.py:407
  289.0 206.8 %collective-permute-start.5 = (bf16[4,192,512]{2,1,0:T(8,128)(2,1)}, bf16[4,192,512]{2,1,0:T(8,128)(2,1)}, u32[]{:S(2)}, u32[]{:S(2)}) collective-permute-start(bf16[4,192,512]{2,1,0:T(8,128)(2,1)} %get-tuple-element.94), channel_id=1, source_target_pairs={{0,4},{4,0},{1,5},{5,1},{2,6},{6,2},{3,7},{7,3}} | collective-permute-start | bytes 2359304 | tf_op jit(solution)/shard_map/ppermute | solution.py:407
Sparse Core Ops, SparseCore 0:
  10.4 22.8 all-gather.11
  35.7 27.2 all-gather.9
  65.3 20.0 all-gather.7
  207.0 37.7 reduce-scatter.5
  264.7 50.5 reduce-scatter.3
  318.4 78.8 reduce-scatter.7

commit v3 on v2

--- a/solution.py
+++ b/solution.py
@@ -2,6 +2,7 @@
 import math
 import jax
 import jax.numpy as jnp
+import numpy as np
 from jax import lax
 from jax.experimental import pallas as pl
 from jax.experimental.pallas import tpu as pltpu
@@ -13,6 +14,7 @@
 D, INNER = 512, 384
 T, E = 384, 192
 PAIRS, BLK = 3, 128
+ROWS = 1568
 ROW_OFF = (0, 128, 384)
 F32, BF = jnp.float32, jnp.bfloat16
 GELU_C = math.sqrt(2.0 / math.pi)
@@ -50,6 +52,10 @@
     d_unit = d_norm_f * gain
     d_act = inv_rms * (d_unit - unit_act * jnp.mean(d_unit * unit_act, axis=-1, keepdims=True))
     return d_act, jnp.sum(d_norm_f * unit_act, axis=0, keepdims=True)
+
+
+def gain_rows(small_ref):
+    return jnp.concatenate([small_ref[row] for row in range(4)], axis=1).astype(F32)
 
 
 def half_masks():
@@ -91,25 +97,27 @@
     return rel, bucket
 
 
-def build_bias(table_ref, bias_ref):
+def build_bias(small_ref, bias_ref):
+    tables = [small_ref[0].astype(F32), small_ref[4].astype(F32)]
     for diag in range(3):
         rel, bucket = bucket_block(diag)
         for head in range(6):
-            row = jnp.broadcast_to(table_ref[head:head + 1, :], (BLK, BLK))
+            pos = 3 + head % 3
+            row = jnp.broadcast_to(tables[head // 3][pos:pos + 1, :], (BLK, BLK))
             vals = jnp.take_along_axis(row, bucket, axis=1, mode="promise_in_bounds")
             bias_ref[head, diag] = jnp.where(rel >= 0, vals, -jnp.inf)
 
 
-def self_fwd(part_ref, pack_ref, gain_ref, table_ref, x_ref, x1_ref, qkv_ref, p_ref, ctx_ref, w_ref, bias_ref):
+def self_fwd(part_ref, pack_ref, small_ref, x_ref, x1_ref, qkv_ref, p_ref, ctx_ref, w_ref, bias_ref):
     @pl.when(pl.program_id(0) == 0)
     def _():
         unpack(pack_ref, w_ref)
-        build_bias(table_ref, bias_ref)
+        build_bias(small_ref, bias_ref)
 
     low, high, _ = half_masks()
     x_in = x_ref[0]
     unit_act, _ = unit_norm(x_in)
-    normed = bf(unit_act * gain_ref[0:1, :])
+    normed = bf(unit_act * gain_rows(small_ref)[0:1])
     qkv_ref[0] = bf(nt(normed, w_ref[:3 * INNER]))
     for pair in range(PAIRS):
         lanes = pl.ds(pair * BLK, BLK)
@@ -135,20 +143,26 @@
     x1_ref[0] = bf(x_in.astype(F32) + nn(ctx_ref[0], w_ref[3 * INNER:]))
 
 
-def cross_mlp(begin, part_ref, pack_ref, mlp_ref, gain_ref, x1_ref, enc_ref, dy_ref, *refs):
+def cross_mlp(begin, part_ref, pack_ref, small_ref, x1_ref, enc_ref, dy_ref, *refs):
     if not begin:
         mlp_in_ref, gain_in_ref, _, *refs = refs
-    y_ref, yfull_ref, dmid_ref, q_ref, kv_ref, p_ref, ctx_ref, dmlp_ref, dgain_ref, w_ref, hid_ref, dpre_ref = refs
+    y_ref, yfull_ref, dmid_ref, q_ref, kv_ref, p_ref, ctx_ref, dmlp_ref, dgain_ref, w_ref, mlp_ref, hid_ref, dpre_ref = refs
 
     @pl.when(pl.program_id(0) == 0)
     def _():
         unpack(pack_ref, w_ref)
+        for half, mat, row, blk in np.ndindex(2, 2, 4, 4):
+            first = 768 + 512 * mat + BLK * blk
+            mlp_ref[half, mat, row * BLK:(row + 1) * BLK, blk * BLK:(blk + 1) * BLK] = pack_ref[4 * half + row, first:first + BLK, :]
+        for half, row in np.ndindex(2, 4):
+            mlp_ref[half, 2, :, row * BLK:(row + 1) * BLK] = pack_ref[4 * half + row, 1792:2304, :]
         dmlp_ref[...] = jnp.zeros_like(dmlp_ref) if begin else mlp_in_ref[...]
         dgain_ref[...] = jnp.zeros_like(dgain_ref) if begin else gain_in_ref[...]
 
     low, high, _ = half_masks()
     unit_act, _ = unit_norm(x1_ref[0])
-    normed = bf(unit_act * gain_ref[1:2, :])
+    gains = gain_rows(small_ref)
+    normed = bf(unit_act * gains[1:2])
     q_ref[0] = bf(nt(normed, w_ref[:INNER]))
     kv_ref[0] = bf(nt(enc_ref[0], w_ref[INNER:3 * INNER]))
     for pair in range(PAIRS):
@@ -169,16 +183,16 @@
     mid_2 = rounded(x1_ref[0].astype(F32) + nn(ctx_ref[0], w_ref[3 * INNER:]))
 
     unit_3, inv_3 = unit_norm(mid_2)
-    gain_3 = gain_ref[2:3, :]
+    gain_3 = gains[2:3]
     normed_3 = bf(unit_3 * gain_3)
     dy = dy_ref[0]
     out = mid_2
     d_norm = jnp.zeros((T, D), F32)
     for half in range(2):
-        wi_0, wi_1, wo_t = [jnp.concatenate([mlp_ref[4 * half + row, mat * BLK:(mat + 1) * BLK] for row in range(4)], axis=0) for mat in range(3)]
+        wi_0, wi_1, w_out = mlp_ref[half, 0], mlp_ref[half, 1], mlp_ref[half, 2]
         pre_0 = rounded(nn(normed_3, wi_0))
         pre_1 = rounded(nn(normed_3, wi_1))
-        d_hid = rounded(nn(dy, wo_t))
+        d_hid = rounded(nt(dy, w_out))
         sq = pre_0 * pre_0
         tanh = jnp.tanh(GELU_C * (pre_0 + 0.044715 * (sq * pre_0)))
         cdf = 0.5 * (1.0 + tanh)
@@ -187,15 +201,16 @@
         hid_ref[...] = bf(gelu * pre_1)
         dpre_ref[:, 0:512] = bf((d_hid * pre_1) * slope)
         dpre_ref[:, 512:1024] = bf(d_hid * gelu)
-        out = out + nt(hid_ref[...], wo_t)
+        out = out + nn(hid_ref[...], w_out)
         d_norm = d_norm + nt(dpre_ref[:, 0:512], wi_0) + nt(dpre_ref[:, 512:1024], wi_1)
         grad_in = tn(normed_3, dpre_ref[...])
-        grad_out = tn(dy, hid_ref[...])
+        grad_out = tn(hid_ref[...], dy)
         for row in range(4):
             rows = slice(row * BLK, (row + 1) * BLK)
-            dmlp_ref[4 * half + row, 0:BLK] += grad_in[rows, 0:512]
-            dmlp_ref[4 * half + row, BLK:2 * BLK] += grad_in[rows, 512:1024]
-            dmlp_ref[4 * half + row, 2 * BLK:3 * BLK] += grad_out[rows]
+            for blk in range(8):
+                cols = slice(blk * BLK, (blk + 1) * BLK)
+                dmlp_ref[4 * half + row, cols, :] += grad_in[rows, cols]
+            dmlp_ref[4 * half + row, 1024:1536, :] += grad_out[:, rows]
     y_ref[0] = bf(out)
     yfull_ref[0] = y_ref[0]
     d_act, d_gain = norm_back(d_norm, unit_3, inv_3, gain_3)
@@ -203,7 +218,7 @@
     dmid_ref[0] = bf(dy.astype(F32) + d_act)
 
 
-def cross_bwd(begin, part_ref, pack_ref, gain_ref, x1_ref, enc_ref, dmid_ref, q_ref, kv_ref, p_ref, ctx_ref, *refs):
+def cross_bwd(begin, part_ref, pack_ref, small_ref, x1_ref, enc_ref, dmid_ref, q_ref, kv_ref, p_ref, ctx_ref, *refs):
     if not begin:
         dw_in_ref, gain_in_ref, _, *refs = refs
     dx1_ref, denc_ref, dencfull_ref, dw_ref, dgain_ref, w_ref, acc_ref, dq_ref, dkv_ref, dctx_ref = refs
@@ -246,7 +261,7 @@
     dencfull_ref[0] = denc_ref[0]
     acc_ref[INNER:3 * INNER] += tn(dkv_ref[...], enc_ref[0])
     unit_act, inv_rms = unit_norm(x1_ref[0])
-    gain = gain_ref[1:2, :]
+    gain = gain_rows(small_ref)[1:2]
     acc_ref[:INNER] += tn(dq_ref[...], bf(unit_act * gain))
     d_act, d_gain = norm_back(nn(dq_ref[...], w_ref[:INNER]), unit_act, inv_rms, gain)
     dgain_ref[...] += jnp.broadcast_to(d_gain, (8, D))
@@ -257,9 +272,34 @@
         repack(acc_ref, dw_ref)
 
 
-def self_bwd(begin, part_ref, pack_ref, gain_ref, x_ref, dmid_ref, qkv_ref, p_ref, ctx_ref, *refs):
+def add_small(dg1_ref, dg2_ref, dg3_ref, dbias_ref, dw_ref):
+    blocks = [bucket_block(diag) for diag in range(3)]
+    buckets = [jnp.where(rel >= 0, bucket, -1) for rel, bucket in blocks]
+    lane = lax.broadcasted_iota(jnp.int32, (8, BLK), 1)
+
+    def one_bucket(bucket_no, sums):
+        rows = []
+        for head in range(6):
+            total = jnp.zeros((BLK, BLK), F32)
+            for diag in range(3):
+                total = total + jnp.where(buckets[diag] == bucket_no, dbias_ref[head, diag], 0.0)
+            rows.append(jnp.sum(total, axis=0, keepdims=True))
+        rows += [jnp.zeros((1, BLK), F32)] * 2
+        per_head = jnp.sum(jnp.concatenate(rows, axis=0), axis=1, keepdims=True)
+        return jnp.where(lane == bucket_no, per_head, sums)
+
+    sums = lax.fori_loop(0, NUM_BUCKETS, one_bucket, jnp.zeros((8, BLK), F32))
+    gains = [ref[...] for ref in (dg1_ref, dg2_ref, dg3_ref)]
+    for half in range(2):
+        for row in range(4):
+            parts = [gain[0:1, row * BLK:(row + 1) * BLK] for gain in gains]
+            parts += [sums[3 * half:3 * half + 3], jnp.zeros((2, BLK), F32)]
+            dw_ref[4 * half + row, 1536:1544, :] = jnp.concatenate(parts, axis=0)
+
+
+def self_bwd(begin, part_ref, pack_ref, small_ref, x_ref, dmid_ref, qkv_ref, p_ref, ctx_ref, *refs):
     if not begin:
-        dw_in_ref, gain_in_ref, bias_in_ref, _, *refs = refs
+        dw_in_ref, gain_in_ref, bias_in_ref, dcross_ref, dg2_ref, dg3_ref, _, *refs = refs
     dx_ref, dxfull_ref, dw_ref, dgain_ref, dbias_ref, w_ref, acc_ref, dqkv_ref, dctx_ref = refs
     step = pl.program_id(0)
 
@@ -307,7 +347,7 @@
                 both = tn(left, rhs[key_blk * BLK:])
                 dqkv_ref[cols, pl.ds(base + pair * BLK, BLK)] = bf(pick_half(both[:BLK], both[BLK:]))
     unit_act, inv_rms = unit_norm(x_ref[0])
-    gain = gain_ref[0:1, :]
+    gain = gain_rows(small_ref)[0:1]
     acc_ref[:3 * INNER] += tn(dqkv_ref[...], bf(unit_act * gain))
     d_act, d_gain = norm_back(nn(dqkv_ref[...], w_ref[:3 * INNER]), unit_act, inv_rms, gain)
     dgain_ref[...] += jnp.broadcast_to(d_gain, (8, D))
@@ -317,28 +357,10 @@
     @pl.when(step == pl.num_programs(0) - 1)
     def _():
         repack(acc_ref, dw_ref)
-
-
-def bucket_sums(dbias_ref, dg1_ref, dg2_ref, dg3_ref, out_ref):
-    blocks = [bucket_block(diag) for diag in range(3)]
-    buckets = [jnp.where(rel >= 0, bucket, -1) for rel, bucket in blocks]
-
-    lane = lax.broadcasted_iota(jnp.int32, (8, BLK), 1)
-
-    def one_bucket(bucket_no, sums):
-        rows = []
-        for head in range(6):
-            total = jnp.zeros((BLK, BLK), F32)
-            for diag in range(3):
-                total = total + jnp.where(buckets[diag] == bucket_no, dbias_ref[head, diag], 0.0)
-            rows.append(jnp.sum(total, axis=0, keepdims=True))
-        rows += [jnp.zeros((1, BLK), F32)] * 2
-        per_head = jnp.sum(jnp.concatenate(rows, axis=0), axis=1, keepdims=True)
-        return jnp.where(lane == bucket_no, per_head, sums)
-
-    out_ref[:, D:] = lax.fori_loop(0, NUM_BUCKETS, one_bucket, jnp.zeros((8, BLK), F32))
-    row = lax.broadcasted_iota(jnp.int32, (8, D), 0)
-    out_ref[:, :D] = jnp.where(row == 0, dg1_ref[...], jnp.where(row == 1, dg2_ref[...], dg3_ref[...]))
+        if not begin:
+            dw_ref[:, 768:1536, :] = dcross_ref[...]
+            dw_ref[:, 1544:ROWS, :] = jnp.zeros((8, ROWS - 1544, BLK), F32)
+            add_small(dgain_ref, dg2_ref, dg3_ref, dbias_ref, dw_ref)
 
 
 def seq_block(first, *dims):
@@ -376,6 +398,10 @@
     )(*args)
 
 
+def stack_cols(weight):
+    return [weight.reshape(BLK, 4, BLK).transpose(1, 0, 2).reshape(512, BLK)]
+
+
 def layer_shard(dec_in, enc_out, grad_out, rel_bias, self_q, self_k, self_v, self_o, cross_q, cross_k, cross_v, cross_o, mlp_wi_0, mlp_wi_1, mlp_wo, norm_self, norm_cross, norm_mlp):
     axes = ("model", "data")
     batch = dec_in.shape[0]
@@ -384,16 +410,12 @@
     part = lax.axis_index("model").astype(jnp.int32).reshape(1)
     rows = (norm_self[None], norm_cross[None], norm_mlp[None], jnp.pad(rel_bias.T, ((0, 0), (0, BLK - NUM_BUCKETS))))
     small = sum(jnp.pad(val, ((pos, 16 - pos - val.shape[0]), (0, 0))) for pos, val in enumerate(rows))
-    small = lax.all_gather(small, axes).astype(F32)
-    gains = small[:4].transpose(1, 0, 2).reshape(16, D)[:8]
-    table = small[:, 3:6].reshape(2, 4, 3, BLK)[:, 0].reshape(6, BLK)
-    table = jnp.pad(table, ((0, 2), (0, 0)))
-    w_self = lax.all_gather(jnp.concatenate([self_q.T, self_k.T, self_v.T, self_o], axis=0), axes)
-    w_cross = lax.all_gather(jnp.concatenate([cross_q.T, cross_k.T, cross_v.T, cross_o], axis=0), axes)
-    w_mlp = lax.all_gather(jnp.concatenate([mlp_wi_0, mlp_wi_1, mlp_wo.T], axis=0), axes)
+    w_self = lax.all_gather(jnp.concatenate([self_q.T, self_k.T, self_v.T, self_o, small], axis=0), axes)
+    w_rest = lax.all_gather(jnp.concatenate([cross_q.T, cross_k.T, cross_v.T, cross_o] + stack_cols(mlp_wi_0) + stack_cols(mlp_wi_1) + [mlp_wo], axis=0), axes)
 
     vmem = pltpu.VMEM
     pack_spec = whole(8, 768, BLK)
+    small_spec = pl.BlockSpec((8, 16, BLK), lambda i, part: (0, 48, 0))
     any_spec = pl.BlockSpec(memory_space=pl.ANY)
     w_scr = vmem((1536, D), BF)
     acc_scr = vmem((1536, D), F32)
@@ -416,22 +438,22 @@
 
     mid_1, qkv, probs, ctx = call(
         self_fwd, seqs, 7_000_000_000,
-        [pack_spec, whole(8, D), whole(8, BLK), arg_block(0, T, D)],
+        [pack_spec, small_spec, arg_block(0, T, D)],
         [seq_out(seqs, (T, D), BF), seq_out(seqs, (T, 3 * INNER), BF), seq_out(seqs, (6, BLK, 768), F32), seq_out(seqs, (T, INNER), BF)],
         [w_scr, vmem((6, 3, BLK, BLK), F32)],
-        (part, w_self, gains, table, dec_in))
+        (part, w_self, w_self, dec_in))
 
     saved, got_y, chain = [], [], ()
     for pos in range(2):
         first = pos * chunk
-        extra = [whole(8, 384, D), whole(8, D), any_spec] if pos else []
+        extra = [whole(8, 1536, BLK), whole(8, D), any_spec] if pos else []
         y_part, y_full, d_mid, q_x, kv_x, probs_x, ctx_x, d_mlp, d_gain_3 = call(
             functools.partial(cross_mlp, pos == 0), chunk, 14_000_000_000,
-            [pack_spec, whole(8, 384, D), whole(8, D), seq_block(first, T, D), arg_block(first, E, D), arg_block(first, T, D)] + extra,
+            [whole(8, 2304, BLK), small_spec, seq_block(first, T, D), arg_block(first, E, D), arg_block(first, T, D)] + extra,
             [seq_out(chunk, (T, D), BF), (arg_block(first, T, D), full_out[T]), seq_out(chunk, (T, D), BF), seq_out(chunk, (T, INNER), BF), seq_out(chunk, (E, 2 * INNER), BF),
-             seq_out(chunk, (6, E, T), F32), seq_out(chunk, (T, INNER), BF), whole_out((8, 384, D), F32), whole_out((8, D), F32)],
-            [w_scr, vmem((T, 512), BF), vmem((T, 1024), BF)],
-            (part, w_cross, w_mlp, gains, mid_1, enc_out, grad_out) + chain, {9: 1} if pos else None)
+             seq_out(chunk, (6, E, T), F32), seq_out(chunk, (T, INNER), BF), whole_out((8, 1536, BLK), F32), whole_out((8, D), F32)],
+            [w_scr, vmem((2, 3, 512, 512), BF), vmem((T, 512), BF), vmem((T, 1024), BF)],
+            (part, w_rest, w_self, mid_1, enc_out, grad_out) + chain, {8: 1} if pos else None)
         chain = (d_mlp, d_gain_3, y_full)
         got_y.append(send(y_part))
         saved.append((d_mid, q_x, kv_x, probs_x, ctx_x))
@@ -443,45 +465,41 @@
         extra = [pack_spec, whole(8, D), any_spec] if pos else []
         d_mid_1, e_part, e_full, d_cross, d_gain_2 = call(
             functools.partial(cross_bwd, pos == 0), chunk, 7_000_000_000,
-            [pack_spec, whole(8, D), seq_block(first, T, D), arg_block(first, E, D), seq_block(0, T, D), seq_block(0, T, INNER), seq_block(0, E, 2 * INNER), seq_block(0, 6, E, T), seq_block(0, T, INNER)] + extra,
+            [pack_spec, small_spec, seq_block(first, T, D), arg_block(first, E, D), seq_block(0, T, D), seq_block(0, T, INNER), seq_block(0, E, 2 * INNER), seq_block(0, 6, E, T), seq_block(0, T, INNER)] + extra,
             [seq_out(chunk, (T, D), BF), seq_out(chunk, (E, D), BF), (arg_block(first, E, D), full_out[E]), whole_out((8, 768, BLK), F32), whole_out((8, D), F32)],
             [w_scr, acc_scr, vmem((T, INNER), BF), vmem((E, 2 * INNER), BF), vmem((T, INNER), BF)],
-            (part, w_cross, gains, mid_1, enc_out) + saved[pos] + chain, {12: 2} if pos else None)
+            (part, w_rest, w_self, mid_1, enc_out) + saved[pos] + chain, {12: 2} if pos else None)
         chain = (d_cross, d_gain_2, e_full)
         got_e.append(send(e_part))
         d_mids.append(d_mid_1)
-    d_cross = scatter(d_cross)
 
     got_x, chain = [], ()
     for pos in range(2):
         first = pos * chunk
-        extra = [pack_spec, whole(8, D), whole(6, 3, BLK, BLK), any_spec] if pos else []
+        extra = [pack_spec, whole(8, D), whole(6, 3, BLK, BLK), pack_spec, whole(8, D), whole(8, D), any_spec] if pos else []
         x_part, x_full, d_self, d_gain_1, d_bias = call(
             functools.partial(self_bwd, pos == 0), chunk, 11_000_000_000,
-            [pack_spec, whole(8, D), arg_block(first, T, D), seq_block(0, T, D), seq_block(first, T, 3 * INNER), seq_block(first, 6, BLK, 768), seq_block(first, T, INNER)] + extra,
-            [seq_out(chunk, (T, D), BF), (arg_block(first, T, D), full_out[T]), whole_out((8, 768, BLK), F32), whole_out((8, D), F32), whole_out((6, 3, BLK, BLK), F32)],
+            [pack_spec, small_spec, arg_block(first, T, D), seq_block(0, T, D), seq_block(first, T, 3 * INNER), seq_block(first, 6, BLK, 768), seq_block(first, T, INNER)] + extra,
+            [seq_out(chunk, (T, D), BF), (arg_block(first, T, D), full_out[T]), whole_out((8, ROWS if pos else 768, BLK), F32), whole_out((8, D), F32), whole_out((6, 3, BLK, BLK), F32)],
             [w_scr, acc_scr, vmem((T, 3 * INNER), BF), vmem((T, INNER), BF)],
-            (part, w_self, gains, dec_in, d_mids[pos], qkv, probs, ctx) + chain, {11: 1} if pos else None)
-        chain = (d_self, d_gain_1, d_bias, x_full)
+            (part, w_self, w_self, dec_in, d_mids[pos], qkv, probs, ctx) + chain, {14: 1} if pos else None)
+        chain = (d_self, d_gain_1, d_bias, d_cross, d_gain_2, d_gain_3, x_full)
         got_x.append(send(x_part))
     d_self = scatter(d_self)
 
-    tiny = pl.pallas_call(bucket_sums, name="bucket_sums", out_shape=shape((8, D + BLK), F32))(d_bias, d_gain_1, d_gain_2, d_gain_3)
-    tiny = lax.psum(tiny, axes)
-    data_no = lax.axis_index("data")
-    gain_grads = lax.dynamic_slice(tiny, (0, data_no * BLK), (3, BLK))
-    gain_grads = (gain_grads[0], gain_grads[1], gain_grads[2])
-    bias_sums = tiny[:, D:D + NUM_BUCKETS]
-    grad_bias = jnp.where(model_no == 0, bias_sums[0:3], bias_sums[3:6]).T
-
+    gain_grads = (d_self[1536], d_self[1537], d_self[1538])
+    grad_bias = d_self[1539:1542, :NUM_BUCKETS].T
     dec_out, grad_enc, grad_dec = place(y_full, got_y), place(e_full, got_e), place(x_full, got_x)
 
     def split_attn(grad_pack):
         mats = [grad_pack[192 * pos:192 * (pos + 1)] for pos in range(4)]
         return mats[0].T, mats[1].T, mats[2].T, mats[3]
 
-    return (dec_out, grad_dec, grad_enc, grad_bias) + split_attn(d_self) + split_attn(d_cross) + (
-        d_mlp[:BLK], d_mlp[BLK:2 * BLK], d_mlp[2 * BLK:].T) + gain_grads
+    def join_cols(rows):
+        return jnp.concatenate([rows[blk * BLK:(blk + 1) * BLK] for blk in range(4)], axis=1)
+
+    return (dec_out, grad_dec, grad_enc, grad_bias) + split_attn(d_self) + split_attn(d_self[768:]) + (
+        join_cols(d_mlp[:512]), join_cols(d_mlp[512:1024]), d_mlp[1024:]) + gain_grads
 
 
 def solution(mesh):

time: 528 us -> 489 us (0.926)
  blocking collectives: 206 us -> 0 us
  waiting for transfers between devices: 33.1 us -> 204 us
    psum x1 -> x0, blocking collectives: 194 us -> none  [layer_shard(): tiny = lax.psum(tiny, axes)]
    ppermute x6, waiting for transfers between devices: 18.4 us -> 187 us  [send(): return lax.ppermute(val, 'model', [(0, 1), (1, 0)])]
    all_gather x1 -> x0, blocking collectives: 12.3 us -> none  [layer_shard(): small = lax.all_gather(small, axes).astype(F32)]
    all_gather x2 -> x1, waiting for transfers between devices: 4.7 us -> 17 us  [layer_shard(): lax.all_gather(jnp.concatenate([self_q.T, self_k.T, self_v.T, self_o, sma...]
    all_gather x1, waiting for transfers between devices: 9.44 us -> 0.02 us  [layer_shard(): lax.all_gather(jnp.concatenate([cross_q.T, cross_k.T, cross_v.T, cross_o]...]
    pallas_call x1 -> x0, Pallas kernels: 7.56 us -> none  [layer_shard(): pl.pallas_call(bucket_sums, name='bucket_sums', out_shape=shape((8, D + B...]
  transfers between devices with their start and end apart: 12 -> 10, of which waited for: 3 -> 3; matrix products, arithmetic and copies ran while one was open for 5% -> 4% of each run, Pallas kernels for 20% -> 29%
where the time goes in v3:
time: 489 us; the launch traced here: 480 us
  Pallas kernels  222 us (45%)
  waiting for transfers between devices  204 us (42%)
  local copies, waits for them, and re-layouts  29.2 us (6%)
  between operations  14.3 us (3%)
  starting transfers between devices  8.48 us (2%)
    pallas_call x7, Pallas kernels, call(): pl.pallas_call(body, out_shape=out_shape, grid_spec=pltpu.PrefetchScalarG...  222 us
    ppermute x6, waiting for transfers between devices, send(): return lax.ppermute(val, 'model', [(0, 1), (1, 0)])  187 us
    all_gather x1, waiting for transfers between devices, layer_shard(): lax.all_gather(jnp.concatenate([self_q.T, self_k.T, self_v.T, self_o, sma...  17 us
    dynamic_update_slice x6, local copies, waits for them, and re-layouts, place(): lax.dynamic_update_slice(full, val, ((1 - model_no) * seqs + pos * chunk,...  11.9 us
  transfers between devices with their start and end apart: 10, of which 3 were waited for; matrix products, arithmetic and copies ran while one was open for 4% of the time, Pallas kernels for 29%

profile of v3, /device:TPU:0, one launch (start us, length us, event | category | flops | bytes accessed | tf_op | source)
XLA Modules:
  0.0 479.9 jit_solution(12623122058815468320)
XLA Ops:
  7.2 0.0 copy-start
  7.2 0.0 all-gather.7.cloned.1.call-start
  7.3 0.8 bitcast_dynamic-update-slice_fusion.2
  8.1 0.8 bitcast_dynamic-update-slice_fusion.1
  8.9 0.8 bitcast_dynamic-update-slice_fusion
  9.7 0.8 constant_dynamic-update-slice_fusion.5
  10.5 0.7 constant_dynamic-update-slice_fusion.4
  11.2 0.0 copy-start.3
  11.2 0.7 copy-done.3
  11.9 0.0 all-gather.7.cloned.1.call-update
  11.9 0.0 all-gather.5.cloned.1.call-start
  12.0 0.8 bitcast_dynamic-update-slice_fusion.5
  12.8 0.8 bitcast_dynamic-update-slice_fusion.4
  13.6 0.8 bitcast_dynamic-update-slice_fusion.3
  14.4 0.8 constant_dynamic-update-slice_fusion.3
  15.2 0.0 copy-done
  15.3 0.9 copy_bitcast_fusion
  16.2 0.9 constant_dynamic-update-slice_fusion
  17.2 0.0 copy-start.2
  17.2 0.8 copy-done.2
  18.0 0.0 all-gather.5.cloned.1.call-update
  18.0 0.0 reduce-scatter.5.cloned.1.call-start
  18.1 17.0 %all-gather.7.cloned.1.call-done = bf16[6272,128]{1,0:T(8,128)(2,1)} async-done(((bf16[784,128]{1,0:T(8,128)(2,1)}), bf16[6272,128]{1,0:T(8,128)(2,1)}) %all-gather.7.cloned.1.call-update) | async-done | bytes 1605648 | tf_op jit(solution)/shard_map/all_gather | solution.py:413
  35.0 38.0 %shard_map.313 = (bf16[8,384,512]{2,1,0:T(8,128)(2,1)}, bf16[8,384,1152]{2,1,0:T(8,128)(2,1)}, f32[8,6,128,768]{3,2,1,0:T(8,128)}, bf16[8,384,384]{2,1,0:T(8,128)(2,1)}) custom-call(s32[1]{0:T(128)} %bitcast.part_ref, bf16[8,784,128]{2,1,0:T(8,128)(2,1)} %bitcast.101, bf16[8,784,128]{2,1,0:T(8,128)(2,1)} %bitcast.102, bf16[16,384,512]{2,1,0:T(8,128)(2,1)} %x_ref.5), custom_call_target="tpu_custom_call" | custom-call | flops 56000000000 | bytes 40000000 | tf_op jit(solution)/shard_map/pallas_call | solution.py:391
  73.0 0.0 all-gather.5.cloned.1.call-done
  73.0 35.1 %shard_map.314 = (bf16[4,384,512]{2,1,0:T(8,128)(2,1)}, bf16[16,384,512]{2,1,0:T(8,128)(2,1)}, bf16[4,384,512]{2,1,0:T(8,128)(2,1)}, bf16[4,384,384]{2,1,0:T(8,1...) custom-call(s32[1]{0:T(128)} %bitcast.part_ref, ...), custom_call_target="tpu_custom_call" | custom-call | flops 56000000000 | bytes 20000000 | tf_op jit(solution)/shard_map/pallas_call | solution.py:391
  108.1 47.4 %shard_map.315 = (bf16[4,384,512]{2,1,0:T(8,128)(2,1)}, bf16[16,384,512]{2,1,0:T(8,128)(2,1)}, bf16[4,384,512]{2,1,0:T(8,128)(2,1)}, bf16[4,384,384]{2,1,0:T(8,1...) custom-call(s32[1]{0:T(128)} %bitcast.part_ref, ...), custom_call_target="tpu_custom_call", output_to_operand_aliasing={{1}: (8, {})} | custom-call | flops 56000000000 | bytes 20000000 | tf_op jit(solution)/shard_map/pallas_call | solution.py:391
  155.5 0.0 reduce-scatter.5.cloned.1.call-update
  155.5 0.0 reduce-scatter.3.cloned.1.call-start
  155.5 18.3 %shard_map.316 = (bf16[4,384,512]{2,1,0:T(8,128)(2,1)}, bf16[4,192,512]{2,1,0:T(8,128)(2,1)}, bf16[16,192,512]{2,1,0:T(8,128)(2,1)}, f32[8,768,128]{2,1,0:T(8,128)}, f32[8,512]{1,0:T(8,128)}) custom-call(s32[1]{0:T(128)} %bitcast.part_ref, bf16[8,2304,128]{2,1,0:T(8,128)(2,1)} %bitcast.99, bf16[8,784,128]{2,1,0:T(8,128)(2,1)} %bitcast.105, ...), custom_call_target="tpu_custom_call" | custom-call | flops 28000000000 | bytes 20000000 | tf_op jit(solution)/shard_map/pallas_call | solution.py:391
  173.9 19.9 %shard_map.317 = (bf16[4,384,512]{2,1,0:T(8,128)(2,1)}, bf16[4,192,512]{2,1,0:T(8,128)(2,1)}, bf16[16,192,512]{2,1,0:T(8,128)(2,1)}, f32[8,768,128]{2,1,0:T(8,128)}, f32[8,512]{1,0:T(8,128)}) custom-call(s32[1]{0:T(128)} %bitcast.part_ref, bf16[8,2304,128]{2,1,0:T(8,128)(2,1)} %bitcast.100, ...), custom_call_target="tpu_custom_call", output_to_operand_aliasing={{2}: (12, {})} | custom-call | flops 28000000000 | bytes 20000000 | tf_op jit(solution)/shard_map/pallas_call | solution.py:391
  193.8 27.2 %shard_map.318 = (bf16[4,384,512]{2,1,0:T(8,128)(2,1)}, bf16[16,384,512]{2,1,0:T(8,128)(2,1)}, f32[8,768,128]{2,1,0:T(8,128)}, f32[8,512]{1,0:T(8,128)}, f32[6,3,128,128]{3,2,1,0:T(8,128)}) custom-call(s32[1]{0:T(128)} %bitcast.part_ref, bf16[8,784,128]{2,1,0:T(8,128)(2,1)} %bitcast.107, bf16[8,784,128]{2,1,0:T(8,128)(2,1)} %bitcast.108, ...), custom_call_target="tpu_custom_call" | custom-call | flops 44000002048 | bytes 20000000 | tf_op jit(solution)/shard_map/pallas_call | solution.py:391
  221.0 36.2 %shard_map.319 = (bf16[4,384,512]{2,1,0:T(8,128)(2,1)}, bf16[16,384,512]{2,1,0:T(8,128)(2,1)}, f32[8,1568,128]{2,1,0:T(8,128)}, f32[8,512]{1,0:T(8,128)}, f32[6,3,128,128]{3,2,1,0:T(8,128)}) custom-call(s32[1]{0:T(128)} %bitcast.part_ref, bf16[8,784,128]{2,1,0:T(8,128)(2,1)} %bitcast.109, ...), custom_call_target="tpu_custom_call", output_to_operand_aliasing={{1}: (14, {})} | custom-call | flops 44000002048 | bytes 20000000 | tf_op jit(solution)/shard_map/pallas_call | solution.py:391
  257.3 0.0 reduce-scatter.3.cloned.1.call-update
  257.3 1.8 collective-permute-start.4
  259.1 0.3 collective-permute-start.2
  259.3 1.8 collective-permute-start.3
  261.1 0.3 collective-permute-start
  261.4 1.8 collective-permute-start.1
  263.1 15.0 %collective-permute-done.4 = bf16[4,192,512]{2,1,0:T(8,128)(2,1)} collective-permute-done((bf16[4,192,512]{2,1,0:T(8,128)(2,1)}, bf16[4,192,512]{2,1,0:T(8,128)(2,1)}, u32[]{:S(2)}, u32[]{:S(2)}) %collective-permute-start.4) | collective-permute-done | bytes 786464 | tf_op jit(solution)/shard_map/ppermute | solution.py:429
  278.1 2.5 collective-permute-start.5
  280.6 2.1 constant_dynamic-update-slice_fusion.7
  282.6 172.2 %collective-permute-done.5 = bf16[4,192,512]{2,1,0:T(8,128)(2,1)} collective-permute-done((bf16[4,192,512]{2,1,0:T(8,128)(2,1)}, bf16[4,192,512]{2,1,0:T(8,128)(2,1)}, u32[]{:S(2)}, u32[]{:S(2)}) %collective-permute-start.5) | collective-permute-done | bytes 786464 | tf_op jit(solution)/shard_map/ppermute | solution.py:429
  454.8 2.1 constant_dynamic-update-slice_fusion.6
  456.9 0.0 collective-permute-done.2
  456.9 2.7 constant_dynamic-update-slice_fusion.9
  459.6 0.0 collective-permute-done.3
  459.6 2.7 constant_dynamic-update-slice_fusion.8
  462.2 0.0 collective-permute-done
  462.2 0.0 copy-start.1
  462.2 1.2 constant_dynamic-update-slice_fusion.11
  463.5 0.0 collective-permute-done.1
  463.5 1.2 constant_dynamic-update-slice_fusion.10
  464.7 0.0 reduce-scatter.5.cloned.1.call-done
  464.7 1.1 slice_bitcast_fusion.12
  465.8 0.8 pad_maximum_fusion
  466.6 1.7 slice_bitcast_fusion
  468.3 0.0 reduce-scatter.3.cloned.1.call-done
  468.3 1.3 slice_bitcast_fusion.17
  469.6 2.1 slice_bitcast_fusion.1
  471.7 1.3 slice_bitcast_fusion.18
  473.0 0.0 copy-done.1
  (3 shorter events, 0.1 us)
Async XLA Ops:
  7.2 8.0 %copy-start = (bf16[128,512]{1,0:T(8,128)(2,1)S(1)}, bf16[128,512]{1,0:T(8,128)(2,1)}, u32[]{:S(2)}) copy-start(bf16[128,512]{1,0:T(8,128)(2,1)} %param.30) | copy-start | bytes 393220
  7.2 27.8 %all-gather.7.cloned.1.call-start = ((), (), s32[]{:S(2)}) async-start(), calls=%async_computation.5 | async-start | bytes 1806336 | tf_op jit(solution)/shard_map/all_gather | solution.py:413
  11.2 0.7 copy-start.3
  11.9 61.1 %all-gather.5.cloned.1.call-start = ((), (), s32[]{:S(2)}) async-start(), calls=%async_computation.4 | async-start | bytes 5308416 | tf_op jit(solution)/shard_map/all_gather | solution.py:414
  17.2 0.8 copy-start.2
  18.0 446.7 %reduce-scatter.5.cloned.1.call-start = ((), (), s32[]{:S(2)}) async-start(), calls=%async_computation.3 | async-start | bytes 7077888 | tf_op jit(solution)/shard_map/reduce_scatter | solution.py:432
  155.5 312.8 %reduce-scatter.3.cloned.1.call-start = ((), (), s32[]{:S(2)}) async-start(), calls=%async_computation.2 | async-start | bytes 7225344 | tf_op jit(solution)/shard_map/reduce_scatter | solution.py:432
  257.3 20.8 %collective-permute-start.4 = (bf16[4,192,512]{2,1,0:T(8,128)(2,1)}, bf16[4,192,512]{2,1,0:T(8,128)(2,1)}, u32[]{:S(2)}, u32[]{:S(2)}) collective-permute-start(bf16[4,192,512]{2,1,0:T(8,128)(2,1)} %get-tuple-element.94), channel_id=1, source_target_pairs={{0,4},{4,0},{1,5},{5,1},{2,6},{6,2},{3,7},{7,3}} | collective-permute-start | bytes 2359304 | tf_op jit(solution)/shard_map/ppermute | solution.py:429
  259.1 197.8 %collective-permute-start.2 = (bf16[4,384,512]{2,1,0:T(8,128)(2,1)}, bf16[4,384,512]{2,1,0:T(8,128)(2,1)}, u32[]{:S(2)}, u32[]{:S(2)}) collective-permute-start(bf16[4,384,512]{2,1,0:T(8,128)(2,1)} %get-tuple-element.91), channel_id=1, source_target_pairs={{0,4},{4,0},{1,5},{5,1},{2,6},{6,2},{3,7},{7,3}} | collective-permute-start | bytes 4718600 | tf_op jit(solution)/shard_map/ppermute | solution.py:429
  259.3 200.2 %collective-permute-start.3 = (bf16[4,384,512]{2,1,0:T(8,128)(2,1)}, bf16[4,384,512]{2,1,0:T(8,128)(2,1)}, u32[]{:S(2)}, u32[]{:S(2)}) collective-permute-start(bf16[4,384,512]{2,1,0:T(8,128)(2,1)} %get-tuple-element.92), channel_id=1, source_target_pairs={{0,4},{4,0},{1,5},{5,1},{2,6},{6,2},{3,7},{7,3}} | collective-permute-start | bytes 4718600 | tf_op jit(solution)/shard_map/ppermute | solution.py:429
  261.1 201.1 %collective-permute-start = (bf16[4,384,512]{2,1,0:T(8,128)(2,1)}, bf16[4,384,512]{2,1,0:T(8,128)(2,1)S(1)}, u32[]{:S(2)}, u32[]{:S(2)}) collective-permute-start(bf16[4,384,512]{2,1,0:T(8,128)(2,1)} %get-tuple-element.63), channel_id=1, source_target_pairs={{0,4},{4,0},{1,5},{5,1},{2,6},{6,2},{3,7},{7,3}} | collective-permute-start | bytes 4718600 | tf_op jit(solution)/shard_map/ppermute | solution.py:429
  261.4 202.1 %collective-permute-start.1 = (bf16[4,384,512]{2,1,0:T(8,128)(2,1)}, bf16[4,384,512]{2,1,0:T(8,128)(2,1)S(1)}, u32[]{:S(2)}, u32[]{:S(2)}) collective-permute-start(bf16[4,384,512]{2,1,0:T(8,128)(2,1)} %get-tuple-element.64), channel_id=1, source_target_pairs={{0,4},{4,0},{1,5},{5,1},{2,6},{6,2},{3,7},{7,3}} | collective-permute-start | bytes 4718600 | tf_op jit(solution)/shard_map/ppermute | solution.py:429
  278.1 176.7 %collective-permute-start.5 = (bf16[4,192,512]{2,1,0:T(8,128)(2,1)}, bf16[4,192,512]{2,1,0:T(8,128)(2,1)}, u32[]{:S(2)}, u32[]{:S(2)}) collective-permute-start(bf16[4,192,512]{2,1,0:T(8,128)(2,1)} %get-tuple-element.95), channel_id=1, source_target_pairs={{0,4},{4,0},{1,5},{5,1},{2,6},{6,2},{3,7},{7,3}} | collective-permute-start | bytes 2359304 | tf_op jit(solution)/shard_map/ppermute | solution.py:429
  462.2 10.7 %copy-start.1 = (bf16[128,512]{1,0:T(8,128)(2,1)S(1)}, bf16[128,512]{1,0:T(8,128)(2,1)}, u32[]{:S(2)}) copy-start(bf16[128,512]{1,0:T(8,128)(2,1)} %param.30) | copy-start | bytes 393220
Sparse Core Ops, SparseCore 0:
  12.1 22.9 all-gather.6
  37.4 33.2 all-gather.4
  155.6 53.4 reduce-scatter.4
  257.4 80.6 reduce-scatter.2
